TPU v7x, 32 devices: a whole 2x2x4 slice. The times are simulated.
32 devices in a mesh: member: 4 (over y, core), lat: 8 (over z, x).
Axes of the slice: x: 2, y: 2, z: 4, core: 2. Of those that a mesh axis runs over, the one named last changes fastest.
Arguments:
- ensemble: float32 [640, 32, 256], P('member', 'lat'), may hold values from -6 to 6
- obs_cell: int32 [32, 128], P(('member', 'lat')), may hold values from 0 to 255
- obs_value: float32 [32, 128], P(('member', 'lat')), may hold values from -8 to 8
- obs_var: float32 [32, 128], P(('member', 'lat')), may hold values from 0.5 to 8
- patch_rows: int32 [32, 2], P(('member', 'lat')), may hold values from 1 to 24, 32 in all within a row
Outputs:
- analysis: float32 [640, 32, 256], P('member', 'lat')
Inputs may be any that keep to these rules, and one draw needn't show every extreme that they name: `patch_rows`: each server's 2 patch lengths sum to 32.
All inputs are finite; a program needn't handle non-finite values. Where the computation divides by a largest or mean magnitude, that divisor is 1e-20 or more.
Results may differ from a plain program's by a relative error of at most 0.0003.
Values sent between devices are 32-bit elements; how exact they have to be, the bound alone decides.
A program may use at most 64 MiB of HBM per device.

v0:
```python
import jax
import jax.numpy as jnp
from jax import lax
from jax.sharding import PartitionSpec as P

STEPS = 4


lat_coeff = 0.4
lon_coeff = 0.05
advect_coeff = 0.1


def with_halo(value, sides, width, wrap):
    for axis, dim in sides:
        size, length = (lax.axis_size(axis), value.shape[dim])
        up = [(i, (i + 1) % size) for i in range(size if wrap else size - 1)]
        down = [(j, i) for i, j in up]
        last = lax.slice_in_dim(value, length - width, length, axis=dim)
        initial = lax.slice_in_dim(value, 0, width, axis=dim)
        before = lax.ppermute(last, axis, up)
        after = lax.ppermute(initial, axis, down)
        value = jnp.concatenate([before, value, after], axis=dim)
    return value


def advance(padded):
    centre = padded[:, 1:-1]
    northern = padded[:, :-2]
    southern = padded[:, 2:]
    eastern = jnp.roll(centre, -1, axis=2)
    western = jnp.roll(centre, 1, axis=2)
    return (
        centre
        + lat_coeff * (northern + southern - 2.0 * centre)
        + lon_coeff * (eastern + western - 2.0 * centre)
        - advect_coeff * centre * (eastern - western)
    )


def observe(states, cell_index, values):
    observed = jnp.take(states, cell_index, axis=1)
    obs_mean = jnp.mean(observed, axis=0)
    return (observed - obs_mean, values - obs_mean)


def localize(obs_rows, rel_cols, first_row, row_count, lat_scale, width_cols):
    lower = first_row.astype(jnp.float32)
    upper = lower + row_count.astype(jnp.float32) - 1.0
    lat_gap = jnp.maximum(jnp.maximum(lower - obs_rows, obs_rows - upper), 0.0) / lat_scale
    lon_gap = jnp.maximum(jnp.maximum(-rel_cols, rel_cols - (width_cols - 1.0)), 0.0) / width_cols
    return jnp.exp(-lat_gap * lat_gap - lon_gap * lon_gap)


def dot3(left, right):
    return jnp.matmul(left, right, precision=lax.Precision.HIGH, preferred_element_type=jnp.float32)


def analyse(states, spread, obs_meta, lengths, width_cols):
    members = states.shape[0]
    cell_total = states.shape[1]
    lat_total = cell_total // width_cols
    near = spread.shape[1]
    state_mean = jnp.mean(states, axis=0)
    anomaly = states - state_mean
    starts = jnp.cumsum(lengths) - lengths
    cell_rows = jnp.arange(cell_total, dtype=jnp.int32) // width_cols
    identity = jnp.eye(members, dtype=jnp.float32)
    products = dot3(spread.T, jnp.concatenate([spread, anomaly], axis=1))
    common, crossed = products[:, :near], products[:, near:]
    innov = obs_meta[0]
    shrink = jnp.zeros((cell_total,), jnp.float32)
    shift = state_mean
    weights_all = jnp.zeros((near, cell_total), jnp.float32)
    for patch in range(lengths.shape[0]):
        weights = (
            localize(
                obs_meta[2],
                obs_meta[3],
                starts[patch],
                lengths[patch],
                lat_total / 4.0,
                float(width_cols),
            )
            / obs_meta[1]
        )
        scale = jnp.sqrt(weights)
        gram_matrix = (members - 1.0) * identity + jnp.dot(
            spread * weights, spread.T, preferred_element_type=jnp.float32
        )
        bound = jnp.max(jnp.sum(jnp.abs(gram_matrix), axis=1))
        alpha = (members - 1.0) / bound
        x = common * scale[:, None] * (scale / bound)[None, :]
        c0 = 2.25 + alpha * (-2.4375 + alpha * (1.6875 + alpha * (-0.5625 + alpha * 0.0625)))
        c1 = -2.4375 + alpha * (3.375 + alpha * (-1.6875 + alpha * 0.25))
        c2 = 1.6875 + alpha * (-1.6875 + alpha * 0.375)
        c3 = -0.5625 + alpha * 0.25
        c4 = 0.0625
        x2 = dot3(x, x)
        x34 = dot3(x2, jnp.concatenate([x, x2], axis=1))
        x3, x4 = x34[:, :near], x34[:, near:]
        low = c2 * x + c3 * x2 + c4 * x3
        high = c1 * x + c2 * x2 + c3 * x3 + c4 * x4
        block = jnp.concatenate([crossed * scale[:, None], (scale * innov)[:, None]], axis=1)
        both = dot3(jnp.concatenate([low, high], axis=0), block)
        b1 = c1 * block + both[:near]
        b2 = c0 * block + both[near:]
        b3 = c0 * b2 + dot3(high, b2)
        mixed = alpha * c0 * b1 + b3
        got = 1.5 * b1 - 0.5 * (
            alpha * c0 * c0 * b1
            + c0 * mixed
            + dot3(high, mixed)
            + alpha * (c1 * b3 + dot3(low, b3))
        )
        base = c0 * (1.5 - 0.5 * alpha * c0 * c0)
        driven = base * block[:, -1] + jnp.sum(x * got[:, -1][None, :], axis=1)
        again = jnp.sum(x * driven[None, :], axis=1)
        mean_part = (
            jnp.sum(block[:, :-1] * (base * driven)[:, None] + got[:, :-1] * again[:, None], axis=0)
            / bound
        )
        cell_mask = (cell_rows >= starts[patch]) & (cell_rows < starts[patch] + lengths[patch])
        root_scale = jnp.sqrt((members - 1.0) / bound)
        shift = shift + jnp.where(cell_mask, mean_part, 0.0)
        shrink = jnp.where(cell_mask, root_scale * base, shrink)
        weights_all = jnp.where(
            cell_mask[None, :], got[:, :-1] * (scale * (root_scale / bound))[:, None], weights_all
        )
    return shift + shrink * anomaly + dot3(spread, weights_all)


def per_device(ensemble, obs_cell, obs_value, obs_var, patch_rows):
    fields = ensemble
    members_dev = fields.shape[0]
    lat_rows = fields.shape[1]
    lon_cells = fields.shape[2]
    lat_count = lax.axis_size("lat")
    member_count = lax.axis_size("member")
    servers = lat_count * member_count
    width_cols = lon_cells // servers
    padded = with_halo(fields, (("lat", 1),), STEPS, False)
    global_rows = (
        lax.axis_index("lat") * lat_rows + jnp.arange(lat_rows + 2 * STEPS, dtype=jnp.int32) - STEPS
    )
    inside = ((global_rows >= 0) & (global_rows < lat_rows * lat_count)).astype(jnp.float32)
    for step_index in range(STEPS):
        padded = advance(padded)
        keeper = inside[step_index + 1 : inside.shape[0] - step_index - 1]
        padded = padded * keeper[None, :, None]
    fields = padded
    blocks = fields.reshape(1, members_dev, lat_rows, lon_cells)
    received = lax.all_to_all(blocks, ("member", "lat"), split_axis=3, concat_axis=0, tiled=True)
    strip = received.reshape(member_count, lat_count, members_dev, lat_rows, width_cols)
    strip = strip.transpose(0, 2, 1, 3, 4).reshape(
        member_count * members_dev, lat_count * lat_rows, width_cols
    )
    members = strip.shape[0]
    lat_total = strip.shape[1]
    states = strip.reshape(members, lat_total * width_cols)
    cell_index = obs_cell[0]
    obs_count = cell_index.shape[0]
    spread, innov = observe(states, cell_index, obs_value[0])
    obs_meta = jnp.stack(
        [
            innov,
            obs_var[0],
            (cell_index // width_cols).astype(jnp.float32),
            (cell_index % width_cols).astype(jnp.float32),
        ]
    )
    near_spread, near_meta = (
        with_halo(spread, ((("member", "lat"), 1),), obs_count, True),
        with_halo(obs_meta, ((("member", "lat"), 1),), obs_count, True),
    )
    shifts = jnp.repeat(jnp.array([-1.0, 0.0, 1.0], jnp.float32), obs_count) * width_cols
    near_meta = jnp.concatenate([near_meta[:3], (near_meta[3] + shifts)[None, :]], axis=0)
    analysed = analyse(states, near_spread, near_meta, patch_rows[0], width_cols)
    analysed = analysed.reshape(members, lat_total, width_cols)
    outgoing = analysed.reshape(member_count, members_dev, lat_count, lat_rows, width_cols)
    outgoing = outgoing.transpose(0, 2, 1, 3, 4).reshape(servers, members_dev, lat_rows, width_cols)
    returned = lax.all_to_all(outgoing, ("member", "lat"), split_axis=0, concat_axis=3, tiled=True)
    return returned.reshape(members_dev, lat_rows, lon_cells)


def solution(mesh):
    in_specs = (
        P("member", "lat", None),
        P(("member", "lat"), None),
        P(("member", "lat"), None),
        P(("member", "lat"), None),
        P(("member", "lat"), None),
    )
    out_specs = P("member", "lat", None)
    return jax.shard_map(
        per_device, mesh=mesh, in_specs=in_specs, out_specs=out_specs, check_vma=False
    )
```

profile of v0, /device:TPU:0, one launch (start us, length us, event | category | flops | bytes accessed | tf_op | source)
XLA Modules:
  0.0 164.4 jit_solution(16774635268156717155)
XLA Ops:
  0.0 1.3 copy.83
  1.3 4.9 %collective-permute-start = (f32[160,4,256]{2,0,1:T(8,128)S(1)}, f32[160,4,256]{2,0,1:T(8,128)S(1)}, u32[]{:S(2)}, u32[]{:S(2)}) collective-permute-start(f32[160,4,256]{2,0,1:T(8,128)S(1)} %copy.83), channel_id=1, source_target_pairs={{0,1},{1,2},{2,3},{3,4},{4,5},{5,6},{6,7},{8,9},{9,10},{10,11},{11... | collective-permute-start | bytes 1966088 | tf_op jit(solution)/shard_map/ppermute | solution.py:21
  6.2 1.3 collective-permute-start.1
  7.8 0.8 reduce-window.9
  8.6 25.5 %collective-permute-done = f32[160,4,256]{2,0,1:T(8,128)S(1)} collective-permute-done((f32[160,4,256]{2,0,1:T(8,128)S(1)}, f32[160,4,256]{2,0,1:T(8,128)S(1)}, u32[]{:S(2)}, u32[]{:S(2)}) %collective-permute-start) | collective-permute-done | bytes 655392 | tf_op jit(solution)/shard_map/ppermute | solution.py:21
  35.3 1.1 fusion.9
  37.0 0.9 fusion.25
  38.4 0.7 fusion.55
  40.1 1.3 copy.86
  41.4 6.6 %all-to-all-start = ((f32[1,160,4,256]{1,2,0,3:T(4,128)}), f32[1,160,4,256]{1,2,0,3:T(4,128)S(1)}, u32[]{:S(2)}, u32[]{:S(2)}) async-start(f32[1,160,4,256]{1,2,0,3:T(4,128)} %copy.86), calls=%async_computation | async-start | bytes 2097152 | tf_op jit(solution)/shard_map/all_to_all | solution.py:153
  48.0 0.6 fusion.135
  49.2 0.6 fusion.134
  54.3 21.2 %all-to-all-done = f32[1,160,4,256]{1,2,0,3:T(4,128)S(1)} async-done(((f32[1,160,4,256]{1,2,0,3:T(4,128)}), f32[1,160,4,256]{1,2,0,3:T(4,128)S(1)}, u32[]{:S(2)}, u32[]{:S(2)}) %all-to-all-start) | async-done | bytes 655392 | tf_op jit(solution)/shard_map/all_to_all | solution.py:153
  75.7 0.7 copy.89
  76.4 0.6 reshape_reshape.6
  77.0 0.8 gather_fusion
  78.2 0.8 collective-permute-start.4
  79.0 4.6 %collective-permute-start.5 = (f32[4,128]{1,0:T(4,128)S(1)}, f32[4,128]{1,0:T(4,128)S(1)}, u32[]{:S(2)}, u32[]{:S(2)}) collective-permute-start(f32[4,128]{1,0:T(4,128)S(1)} %pad_maximum_fusion.22), channel_id=1, source_target_pairs={{1,0},{2,1},{3,2},{4,3},{5,4},{6,5},{7,6},{8,7},{9,8},{10,9},{11,1... | collective-permute-start | bytes 6152 | tf_op jit(solution)/shard_map/ppermute | solution.py:22
  83.7 5.3 %collective-permute-start.3 = (f32[640,128]{1,0:T(8,128)S(1)}, f32[640,128]{1,0:T(8,128)}, u32[]{:S(2)}, u32[]{:S(2)}) collective-permute-start(f32[640,128]{1,0:T(8,128)S(1)} %subtract_bitcast_fusion), channel_id=1, source_target_pairs={{1,0},{2,1},{3,2},{4,3},{5,4},{6,5},{7,6},{8,7},{9,8},{10,9},{11,1... | collective-permute-start | bytes 983048 | tf_op jit(solution)/shard_map/ppermute | solution.py:22
  90.4 6.6 %collective-permute-done.2 = f32[640,128]{1,0:T(8,128)S(1)} collective-permute-done((f32[640,128]{1,0:T(8,128)S(1)}, f32[640,128]{1,0:T(8,128)S(1)}, u32[]{:S(2)}, u32[]{:S(2)}) %collective-permute-start.2) | collective-permute-done | bytes 327712 | tf_op jit(solution)/shard_map/ppermute | solution.py:21
  97.0 2.5 %collective-permute-done.3 = f32[640,128]{1,0:T(8,128)} collective-permute-done((f32[640,128]{1,0:T(8,128)S(1)}, f32[640,128]{1,0:T(8,128)}, u32[]{:S(2)}, u32[]{:S(2)}) %collective-permute-start.3) | collective-permute-done | bytes 327712 | tf_op jit(solution)/shard_map/ppermute | solution.py:22
  99.5 1.8 %fusion.3 = f32[640]{0:T(1024)S(1)} fusion(f32[640,128]{1,0:T(8,128)} %collective-permute-done.3, f32[640,128]{1,0:T(8,128)S(1)} %subtract_bitcast_fusion, f32[640,128]{1,0:T(8,128)S(1)} %collective-permute-done.2, f32[384]{0:T(512)S(1)} %get-tuple-element.25), kind=kOutput, calls=%fused_computation.6 | convolution fusion | flops 317848960 | bytes 987136 | tf_op jit(solution)/shard_map/dot_general | solution.py:88
  101.3 0.7 reduce_max.19
  102.7 1.8 %fusion.1 = f32[640]{0:T(1024)S(1)} fusion(f32[640,128]{1,0:T(8,128)} %collective-permute-done.3, f32[640,128]{1,0:T(8,128)S(1)} %subtract_bitcast_fusion, f32[640,128]{1,0:T(8,128)S(1)} %collective-permute-done.2, f32[384]{0:T(512)S(1)} %get-tuple-element.53), kind=kOutput, calls=%fused_computation.4 | convolution fusion | flops 317848960 | bytes 987136 | tf_op jit(solution)/shard_map/dot_general | solution.py:88
  104.5 0.6 reduce_max.18
  107.2 0.7 divide_reduce_fusion
  107.9 0.6 divide_reduce_fusion.1
  108.6 0.7 broadcast_multiply_fusion.1
  109.3 2.6 %fusion.10 = f32[384,640]{1,0:T(8,128)S(1)} fusion(f32[640,256]{1,0:T(8,128)S(1)} %broadcast_subtract_fusion, f32[640,128]{1,0:T(8,128)} %collective-permute-done.3, f32[640,128]{1,0:T(8,128)S(1)} %subtract_bitcast_fusion, f32[640,128]{1,0:T(8,128)S(1)} %collective-permute-done.2), kind=kOutput, calls=%fused_computation.16 | convolution fusion | flops 945438720 | bytes 2621440 | tf_op jit(solution)/shard_map/dot_general | solution.py:56
  112.3 0.7 fusion.136
  113.0 0.8 copy-done
  113.9 2.1 %fusion.34 = f32[384,768]{1,0:T(8,128)} fusion(f32[384,384]{1,0:T(8,128)S(1)} %fusion.136, f32[384,384]{1,0:T(8,128)S(1)} %get-tuple-element.47), kind=kOutput, calls=%fused_computation.51 | convolution fusion | flops 679772160 | bytes 2359296 | tf_op jit(solution)/shard_map/dot_general | solution.py:56
  116.0 0.7 fusion.137
  116.7 1.1 fusion.42
  118.4 1.3 fusion.46
  119.6 0.8 convolution_add_fusion.3
  120.4 0.7 fusion.33
  121.2 1.0 fusion.32
  122.1 0.8 copy-done.3
  123.2 1.5 fusion.38
  124.7 0.8 convolution_add_fusion.6
  125.5 0.7 fusion.29
  126.3 0.9 fusion.28
  128.4 2.4 %fusion.104 = (f32[256]{0:T(256)S(1)}, pred[256]{0:T(512)(128)(4,1)S(1)}, pred[256]{0:T(512)(128)(4,1)S(1)}) fusion(f32[256]{0:T(256)S(1)} %add_reduce_fusion, f32[256]{0:T(256)S(1)} %copy-done.17, f32[256]{0:T(256)S(1)} %add_reduce_fusion.1, f32[]{:T(128)} %reduce_max.19, f32[]{:T(128)} %reduce_max.18, s32[]{:T(128)S(6)} %add.404, s32[]{:T(128)} %bitcast.8, ...), kind=kLoop, calls=%fused_computation.203 | loop fusion | flops 5120 | bytes 4632 | tf_op jit(solution)/shard_map/add | solution.py:125
  130.9 1.8 %convolution_add_fusion = f32[640,256]{1,0:T(8,128)S(1)} fusion(f32[640,256]{1,0:T(8,128)S(1)} %copy-done.7, f32[640,128]{1,0:T(8,128)} %collective-permute-done.3, f32[640,128]{1,0:T(8,128)S(1)} %copy-done.9, f32[640,128]{1,0:T(8,128)S(1)} %copy-done.11, f32[384,257]{1,0:T(8,128)S(1)} %copy-done.4, f32[384,257]{1,0:T(8,128)S(1)} %fusion.28, ...), kind=kOutput, calls=%fused_computation.36 | convolution fusion | flops 378863616 | bytes 3087360 | tf_op jit(solution)/shard_map/dot_general | solution.py:56
  132.9 0.7 reshape_reshape.7
  133.9 29.2 %all_to_all.30 = f32[32,160,4,8]{1,3,2,0:T(8,128)S(1)} all-to-all(f32[32,160,4,8]{1,3,2,0:T(8,128)S(1)} %bitcast.110), channel_id=1, replica_groups=mesh['member'=4,'lat'=8] {'member','lat'}, dimensions={0} | all-to-all | bytes 1310720 | tf_op jit(solution)/shard_map/all_to_all | solution.py:182
  163.2 1.1 copy.107
  (112 shorter events, 8.3 us)
Async XLA Ops:
  0.0 34.2 %copy-start.5 = (f32[160,4,256]{2,1,0:T(4,128)S(1)}, f32[160,4,256]{2,1,0:T(4,128)}, u32[]{:S(2)}) copy-start(f32[160,4,256]{2,1,0:T(4,128)} %param.6) | copy-start | bytes 1966084
  1.3 32.9 %collective-permute-start = (f32[160,4,256]{2,0,1:T(8,128)S(1)}, f32[160,4,256]{2,0,1:T(8,128)S(1)}, u32[]{:S(2)}, u32[]{:S(2)}) collective-permute-start(f32[160,4,256]{2,0,1:T(8,128)S(1)} %copy.83), channel_id=1, source_target_pairs={{0,1},{1,2},{2,3},{3,4},{4,5},{5,6},{6,7},{8,9},{9,10},{10,11},{11... | collective-permute-start | bytes 1966088 | tf_op jit(solution)/shard_map/ppermute | solution.py:21
  6.2 28.2 %collective-permute-start.1 = (f32[160,4,256]{2,0,1:T(8,128)S(1)}, f32[160,4,256]{2,0,1:T(8,128)S(1)}, u32[]{:S(2)}, u32[]{:S(2)}) collective-permute-start(f32[160,4,256]{2,0,1:T(8,128)S(1)} %copy.83), channel_id=1, source_target_pairs={{1,0},{2,1},{3,2},{4,3},{5,4},{6,5},{7,6},{9,8},{10,9},{11,10},{12... | collective-permute-start | bytes 1966088 | tf_op jit(solution)/shard_map/ppermute | solution.py:22
  40.0 8.0 %copy-start.21 = (s32[1,2]{1,0:T(1,128)S(1)}, s32[1,2]{1,0:T(1,128)}, u32[]{:S(2)}) copy-start(s32[1,2]{1,0:T(1,128)} %param.10) | copy-start | bytes 28
  40.0 14.1 %copy-start.23 = (s32[1,128]{1,0:T(1,128)S(1)}, s32[1,128]{1,0:T(1,128)}, u32[]{:S(2)}) copy-start(s32[1,128]{1,0:T(1,128)} %param.7) | copy-start | bytes 1540
  40.1 14.1 %copy-start.20 = (f32[3]{0:T(128)S(1)}, f32[3]{0:T(128)}, u32[]{:S(2)}) copy-start(f32[3]{0:T(128)} %constant.157) | copy-start | bytes 40
  41.4 34.1 %all-to-all-start = ((f32[1,160,4,256]{1,2,0,3:T(4,128)}), f32[1,160,4,256]{1,2,0,3:T(4,128)S(1)}, u32[]{:S(2)}, u32[]{:S(2)}) async-start(f32[1,160,4,256]{1,2,0,3:T(4,128)} %copy.86), calls=%async_computation | async-start | bytes 2097152 | tf_op jit(solution)/shard_map/all_to_all | solution.py:153
  77.0 1.1 copy-start.24
  77.0 1.1 copy-start.22
  78.2 11.6 %collective-permute-start.4 = (f32[4,128]{1,0:T(4,128)S(1)}, f32[4,128]{1,0:T(4,128)S(1)}, u32[]{:S(2)}, u32[]{:S(2)}) collective-permute-start(f32[4,128]{1,0:T(4,128)S(1)} %pad_maximum_fusion.22), channel_id=1, source_target_pairs={{0,1},{1,2},{2,3},{3,4},{4,5},{5,6},{6,7},{7,8},{8,9},{9,10},{10,1... | collective-permute-start | bytes 6152 | tf_op jit(solution)/shard_map/ppermute | solution.py:21
  79.0 10.7 %collective-permute-start.5 = (f32[4,128]{1,0:T(4,128)S(1)}, f32[4,128]{1,0:T(4,128)S(1)}, u32[]{:S(2)}, u32[]{:S(2)}) collective-permute-start(f32[4,128]{1,0:T(4,128)S(1)} %pad_maximum_fusion.22), channel_id=1, source_target_pairs={{1,0},{2,1},{3,2},{4,3},{5,4},{6,5},{7,6},{8,7},{9,8},{10,9},{11,1... | collective-permute-start | bytes 6152 | tf_op jit(solution)/shard_map/ppermute | solution.py:22
  83.6 25.7 %copy-start.8 = (f32[640,128]{1,0:T(8,128)}, f32[640,128]{1,0:T(8,128)S(1)}, u32[]{:S(2)}) copy-start(f32[640,128]{1,0:T(8,128)S(1)} %subtract_bitcast_fusion) | copy-start | bytes 983044
  83.6 13.4 %collective-permute-start.2 = (f32[640,128]{1,0:T(8,128)S(1)}, f32[640,128]{1,0:T(8,128)S(1)}, u32[]{:S(2)}, u32[]{:S(2)}) collective-permute-start(f32[640,128]{1,0:T(8,128)S(1)} %subtract_bitcast_fusion), channel_id=1, source_target_pairs={{0,1},{1,2},{2,3},{3,4},{4,5},{5,6},{6,7},{7,8},{8,9},{9,10},{10,1... | collective-permute-start | bytes 983048 | tf_op jit(solution)/shard_map/ppermute | solution.py:21
  83.7 15.8 %collective-permute-start.3 = (f32[640,128]{1,0:T(8,128)S(1)}, f32[640,128]{1,0:T(8,128)}, u32[]{:S(2)}, u32[]{:S(2)}) collective-permute-start(f32[640,128]{1,0:T(8,128)S(1)} %subtract_bitcast_fusion), channel_id=1, source_target_pairs={{1,0},{2,1},{3,2},{4,3},{5,4},{6,5},{7,6},{8,7},{9,8},{10,9},{11,1... | collective-permute-start | bytes 983048 | tf_op jit(solution)/shard_map/ppermute | solution.py:22
  89.6 0.6 copy-start.16
  89.7 19.6 %copy-start.6 = (f32[640,256]{1,0:T(8,128)}, f32[640,256]{1,0:T(8,128)S(1)}, u32[]{:S(2)}) copy-start(f32[640,256]{1,0:T(8,128)S(1)} %broadcast_subtract_fusion) | copy-start | bytes 1966084
  89.8 18.1 %copy-start.12 = (f32[1,384]{1,0:T(1,128)}, f32[1,384]{1,0:T(1,128)S(1)}, u32[]{:S(2)}) copy-start(f32[1,384]{1,0:T(1,128)S(1)} %get-tuple-element.54) | copy-start | bytes 4612
  90.4 16.8 %copy-start.14 = (f32[1,384]{1,0:T(1,128)}, f32[1,384]{1,0:T(1,128)S(1)}, u32[]{:S(2)}) copy-start(f32[1,384]{1,0:T(1,128)S(1)} %get-tuple-element.26) | copy-start | bytes 4612
  97.0 12.3 %copy-start.10 = (f32[640,128]{1,0:T(8,128)}, f32[640,128]{1,0:T(8,128)S(1)}, u32[]{:S(2)}) copy-start(f32[640,128]{1,0:T(8,128)S(1)} %collective-permute-done.2) | copy-start | bytes 983044
  113.0 0.8 copy-start
  116.0 1.9 %copy-start.1 = (f32[384,384]{1,0:T(8,128)S(1)}, f32[384,384]{1,0:T(8,128)}, u32[]{:S(2)}) copy-start(f32[384,384]{1,0:T(8,128)} %copy-done) | copy-start | bytes 1769476
  116.0 1.9 %copy-start.2 = (f32[384,768]{1,0:T(8,128)S(1)}, f32[384,768]{1,0:T(8,128)}, u32[]{:S(2)}) copy-start(f32[384,768]{1,0:T(8,128)} %fusion.34) | copy-start | bytes 3538948
  122.1 0.8 copy-start.3
  126.2 1.3 copy-start.13
  126.2 1.3 copy-start.15
  127.2 1.1 copy-start.4
  127.3 1.1 copy-start.17
  127.4 3.5 %copy-start.7 = (f32[640,256]{1,0:T(8,128)S(1)}, f32[640,256]{1,0:T(8,128)}, u32[]{:S(2)}) copy-start(f32[640,256]{1,0:T(8,128)} %copy-done.6) | copy-start | bytes 1966084
  127.4 3.5 %copy-start.9 = (f32[640,128]{1,0:T(8,128)S(1)}, f32[640,128]{1,0:T(8,128)}, u32[]{:S(2)}) copy-start(f32[640,128]{1,0:T(8,128)} %copy-done.8) | copy-start | bytes 983044
  127.4 3.5 %copy-start.11 = (f32[640,128]{1,0:T(8,128)S(1)}, f32[640,128]{1,0:T(8,128)}, u32[]{:S(2)}) copy-start(f32[640,128]{1,0:T(8,128)} %copy-done.10) | copy-start | bytes 983044
  127.4 3.5 %copy-start.18 = (f32[384]{0:T(512)S(1)}, f32[384]{0:T(512)}, u32[]{:S(2)}) copy-start(f32[384]{0:T(512)} %get-tuple-element.12) | copy-start | bytes 4612
  127.4 3.5 %copy-start.19 = (f32[384]{0:T(512)S(1)}, f32[384]{0:T(512)}, u32[]{:S(2)}) copy-start(f32[384]{0:T(512)} %get-tuple-element.56) | copy-start | bytes 4612
where the time goes:
time: 165 us; the launch traced here: 164 us
  waiting for transfers between devices  55.9 us (34%)
  blocking collectives  29.2 us (18%)
  starting transfers between devices  23.6 us (14%)
  matrix products  20.3 us (12%)
  local copies, waits for them, and re-layouts  14.7 us (9%)
  other arithmetic  12.1 us (7%)
  between operations  8.58 us (5%)
    ppermute x3, waiting for transfers between devices, with_halo(): before = lax.ppermute(last, axis, up)  32.1 us
    all_to_all x1, blocking collectives, per_device(): lax.all_to_all(outgoing, ('member', 'lat'), split_axis=0, concat_axis=3,...  29.2 us
    all_to_all x1, waiting for transfers between devices, per_device(): lax.all_to_all(blocks, ('member', 'lat'), split_axis=3, concat_axis=0, ti...  21.2 us
    dot_general x14, matrix products, dot3(): jnp.matmul(left, right, precision=lax.Precision.HIGH, preferred_element_t...  16.7 us
    ppermute x3, starting transfers between devices, with_halo(): after = lax.ppermute(initial, axis, down)  11.2 us
    all_to_all x1, starting transfers between devices, per_device(): lax.all_to_all(blocks, ('member', 'lat'), split_axis=3, concat_axis=0, ti...  6.62 us
    ppermute x3, starting transfers between devices, with_halo(): before = lax.ppermute(last, axis, up)  5.8 us
    unnamed x54, local copies, waits for them, and re-layouts  3.6 us
  transfers between devices with their start and end apart: 7, of which 4 were waited for; matrix products, arithmetic and copies ran while one was open for 2% of the time, Pallas kernels for 0%

commit v1 on v0

--- a/solution.py
+++ b/solution.py
@@ -1,6 +1,10 @@
+import functools
+
 import jax
 import jax.numpy as jnp
 from jax import lax
+from jax.experimental import pallas as pl
+from jax.experimental.pallas import tpu as pltpu
 from jax.sharding import PartitionSpec as P
 
 STEPS = 4
@@ -57,16 +61,16 @@
 
 
 def analyse(states, spread, obs_meta, lengths, width_cols):
-    members = states.shape[0]
-    cell_total = states.shape[1]
+    members = states.shape[1]
+    cell_total = states.shape[0]
     lat_total = cell_total // width_cols
-    near = spread.shape[1]
-    state_mean = jnp.mean(states, axis=0)
-    anomaly = states - state_mean
+    near = spread.shape[0]
+    state_mean = jnp.mean(states, axis=1)
+    anomaly = states - state_mean[:, None]
     starts = jnp.cumsum(lengths) - lengths
     cell_rows = jnp.arange(cell_total, dtype=jnp.int32) // width_cols
     identity = jnp.eye(members, dtype=jnp.float32)
-    products = dot3(spread.T, jnp.concatenate([spread, anomaly], axis=1))
+    products = dot3(spread, jnp.concatenate([spread, anomaly], axis=0).T)
     common, crossed = products[:, :near], products[:, near:]
     innov = obs_meta[0]
     shrink = jnp.zeros((cell_total,), jnp.float32)
@@ -86,7 +90,7 @@
         )
         scale = jnp.sqrt(weights)
         gram_matrix = (members - 1.0) * identity + jnp.dot(
-            spread * weights, spread.T, preferred_element_type=jnp.float32
+            (spread * weights[:, None]).T, spread, preferred_element_type=jnp.float32
         )
         bound = jnp.max(jnp.sum(jnp.abs(gram_matrix), axis=1))
         alpha = (members - 1.0) / bound
@@ -127,10 +131,10 @@
         weights_all = jnp.where(
             cell_mask[None, :], got[:, :-1] * (scale * (root_scale / bound))[:, None], weights_all
         )
-    return shift + shrink * anomaly + dot3(spread, weights_all)
-
-
-def per_device(ensemble, obs_cell, obs_value, obs_var, patch_rows):
+    return shift[:, None] + shrink[:, None] * anomaly + dot3(weights_all.T, spread)
+
+
+def plain_device(ensemble, obs_cell, obs_value, obs_var, patch_rows):
     fields = ensemble
     members_dev = fields.shape[0]
     lat_rows = fields.shape[1]
@@ -175,12 +179,339 @@
     )
     shifts = jnp.repeat(jnp.array([-1.0, 0.0, 1.0], jnp.float32), obs_count) * width_cols
     near_meta = jnp.concatenate([near_meta[:3], (near_meta[3] + shifts)[None, :]], axis=0)
-    analysed = analyse(states, near_spread, near_meta, patch_rows[0], width_cols)
+    analysed = analyse(states.T, near_spread.T, near_meta, patch_rows[0], width_cols).T
     analysed = analysed.reshape(members, lat_total, width_cols)
     outgoing = analysed.reshape(member_count, members_dev, lat_count, lat_rows, width_cols)
     outgoing = outgoing.transpose(0, 2, 1, 3, 4).reshape(servers, members_dev, lat_rows, width_cols)
     returned = lax.all_to_all(outgoing, ("member", "lat"), split_axis=0, concat_axis=3, tiled=True)
     return returned.reshape(members_dev, lat_rows, lon_cells)
+
+
+LANES = 128
+
+
+def group_of(place):
+    return place + (place % 4) // 2 * (1 - 2 * (place % 2))
+
+
+def turn_of(group, index, size):
+    return (group % 2) * (size - 1 - index) + (1 - group % 2) * index
+
+
+def server_of(member, lat, member_count):
+    group = group_of(lat)
+    return member_count * group + turn_of(group, member, member_count)
+
+
+def host_of(server, member_count):
+    group = server // member_count
+    return turn_of(group, server % member_count, member_count), group_of(group)
+
+
+def exchange_kernel(count, place, source, target, me_of, x_ref, o_ref, send_sem, recv_sem, own_sem):
+    me = me_of()
+    barrier = pltpu.get_barrier_semaphore()
+
+    def greet(step, carry):
+        pl.semaphore_signal(barrier, inc=1, device_id=place(lax.rem(me + step, count)), device_id_type=pl.DeviceIdType.MESH)
+        return carry
+
+    lax.fori_loop(1, count, greet, 0)
+    own = pltpu.make_async_copy(x_ref.at[source(me)], o_ref.at[target(me)], own_sem)
+    own.start()
+    pl.semaphore_wait(barrier, count - 1)
+
+    def sending(step):
+        other = lax.rem(me + step, count)
+        return pltpu.make_async_remote_copy(
+            src_ref=x_ref.at[source(other)],
+            dst_ref=o_ref.at[target(me)],
+            send_sem=send_sem.at[step],
+            recv_sem=recv_sem.at[step],
+            device_id=place(other),
+            device_id_type=pl.DeviceIdType.MESH,
+        )
+
+    def arriving(step):
+        other = lax.rem(me + count - step, count)
+        return pltpu.make_async_remote_copy(
+            src_ref=x_ref.at[source(other)],
+            dst_ref=o_ref.at[target(other)],
+            send_sem=send_sem.at[step],
+            recv_sem=recv_sem.at[step],
+            device_id=place(other),
+            device_id_type=pl.DeviceIdType.MESH,
+        )
+
+    def start(step, carry):
+        sending(step).start()
+        return carry
+
+    def finish(step, carry):
+        arriving(step).wait_recv()
+        sending(step).wait_send()
+        return carry
+
+    lax.fori_loop(1, count, start, 0)
+    own.wait()
+    lax.fori_loop(1, count, finish, 0)
+
+
+def exchange(blocks, count, place, source, target, me_of, number):
+    moved = blocks.size * 4
+    return pl.pallas_call(
+        functools.partial(exchange_kernel, count, place, source, target, me_of),
+        out_shape=jax.ShapeDtypeStruct(blocks.shape, jnp.float32),
+        in_specs=[pl.BlockSpec(memory_space=pltpu.VMEM)],
+        out_specs=pl.BlockSpec(memory_space=pltpu.VMEM),
+        scratch_shapes=[
+            pltpu.SemaphoreType.DMA((count,)),
+            pltpu.SemaphoreType.DMA((count,)),
+            pltpu.SemaphoreType.DMA,
+        ],
+        compiler_params=pltpu.CompilerParams(collective_id=number, has_side_effects=True),
+        cost_estimate=pl.CostEstimate(flops=0, bytes_accessed=40 * moved, transcendentals=0),
+    )(blocks)
+
+
+def ring_kernel(member_count, lat_count, x_ref, before_ref, after_ref, send_sem, recv_sem):
+    servers = member_count * lat_count
+    me = server_of(lax.axis_index("member"), lax.axis_index("lat"), member_count)
+
+    def place(server):
+        member, lat = host_of(server, member_count)
+        return {"member": member, "lat": lat}
+
+    up, down = place(lax.rem(me + 1, servers)), place(lax.rem(me + servers - 1, servers))
+    barrier = pltpu.get_barrier_semaphore()
+    for beside in (up, down):
+        pl.semaphore_signal(barrier, inc=1, device_id=beside, device_id_type=pl.DeviceIdType.MESH)
+    pl.semaphore_wait(barrier, 2)
+    copies = []
+    for side, (beside, landing) in enumerate(((up, before_ref), (down, after_ref))):
+        copy = pltpu.make_async_remote_copy(
+            src_ref=x_ref,
+            dst_ref=landing,
+            send_sem=send_sem.at[side],
+            recv_sem=recv_sem.at[side],
+            device_id=beside,
+            device_id_type=pl.DeviceIdType.MESH,
+        )
+        copy.start()
+        copies.append(copy)
+    for copy in copies:
+        copy.wait()
+
+
+def ring(own, member_count, lat_count, number):
+    shape = jax.ShapeDtypeStruct(own.shape, jnp.float32)
+    vmem = pl.BlockSpec(memory_space=pltpu.VMEM)
+    return pl.pallas_call(
+        functools.partial(ring_kernel, member_count, lat_count),
+        out_shape=(shape, shape),
+        in_specs=[vmem],
+        out_specs=(vmem, vmem),
+        scratch_shapes=[pltpu.SemaphoreType.DMA((2,)), pltpu.SemaphoreType.DMA((2,))],
+        compiler_params=pltpu.CompilerParams(collective_id=number, has_side_effects=True),
+        cost_estimate=pl.CostEstimate(flops=0, bytes_accessed=100 * own.size, transcendentals=0),
+    )(own)
+
+
+def forecast_kernel(strips, width_cols, x_ref, o_ref):
+    lat_count, packed, cells, _ = x_ref.shape
+    lat_rows = packed - 1
+    piece = LANES // lat_rows
+    main = x_ref[:, :lat_rows].reshape(lat_count * lat_rows, cells, LANES)
+    rest = x_ref[:, lat_rows]
+    lane = lax.broadcasted_iota(jnp.int32, rest.shape, 2)
+
+    def step(centre, north, south):
+        east = pltpu.roll(centre, cells - 1, axis=1)
+        west = pltpu.roll(centre, 1, axis=1)
+        return (
+            centre
+            + lat_coeff * (north + south - 2.0 * centre)
+            + lon_coeff * (east + west - 2.0 * centre)
+            - advect_coeff * centre * (east - west)
+        )
+
+    empty = jnp.zeros((1, cells, LANES), jnp.float32)
+    for _ in range(STEPS):
+        main_north = jnp.concatenate([empty, main[:-1]], axis=0)
+        main_south = jnp.concatenate([main[1:], empty], axis=0)
+        lower = pltpu.roll(rest, piece, axis=2)
+        upper = pltpu.roll(rest, LANES - piece, axis=2)
+        rest_north = jnp.where(lane < piece, jnp.concatenate([empty, lower[:-1]], axis=0), lower)
+        rest_south = jnp.where(lane >= LANES - piece, jnp.concatenate([upper[1:], empty], axis=0), upper)
+        main = step(main, main_north, main_south)
+        rest = step(rest, rest_north, rest_south)
+    main = pltpu.roll(main, cells - STEPS, axis=1)
+    rest = pltpu.roll(rest, cells - STEPS, axis=1)
+    for strip in range(strips):
+        own = slice(strip * width_cols, (strip + 1) * width_cols)
+        o_ref[strip, :, :lat_rows] = main[:, own].reshape(lat_count, lat_rows, width_cols, LANES)
+        o_ref[strip, :, lat_rows] = rest[:, own]
+
+
+def gather_kernel(x_ref, o_ref):
+    member_count, lat_count, packed, width_cols, _ = x_ref.shape
+    lat_rows = packed - 1
+    piece = LANES // lat_rows
+    cells = lat_count * lat_rows * width_cols
+    for member in range(member_count):
+        o_ref[:, member * LANES : (member + 1) * LANES] = x_ref[member, :, :lat_rows].reshape(cells, LANES)
+    rest = [x_ref[member, :, lat_rows] for member in range(member_count)]
+    part = lax.broadcasted_iota(jnp.int32, rest[0].shape, 2) // piece
+    rows = []
+    for row in range(lat_rows):
+        total = rest[row]
+        for member in range(member_count):
+            if member != row:
+                moved = pltpu.roll(rest[member], (member - row) * piece % LANES, axis=2)
+                total = jnp.where(part == member, moved, total)
+        rows.append(total)
+    o_ref[:, member_count * LANES :] = jnp.stack(rows, axis=1).reshape(cells, LANES)
+
+
+def scatter_kernel(lat_count, width_cols, x_ref, o_ref):
+    member_count = x_ref.shape[1] // LANES - 1
+    lat_rows = o_ref.shape[1] - 1
+    piece = LANES // lat_rows
+    held = x_ref[:, member_count * LANES :].reshape(lat_count, lat_rows, width_cols, LANES)
+    part = lax.broadcasted_iota(jnp.int32, held[:, 0].shape, 2) // piece
+    for member in range(member_count):
+        own = slice(member * lat_count, (member + 1) * lat_count)
+        o_ref[own, :lat_rows] = x_ref[:, member * LANES : (member + 1) * LANES].reshape(
+            lat_count, lat_rows, width_cols, LANES
+        )
+        total = held[:, member]
+        for row in range(lat_rows):
+            if row != member:
+                moved = pltpu.roll(held[:, row], (row - member) * piece % LANES, axis=2)
+                total = jnp.where(part == row, moved, total)
+        o_ref[own, lat_rows] = total
+
+
+def local(kernel, shape, *operands):
+    vmem = pl.BlockSpec(memory_space=pltpu.VMEM)
+    return pl.pallas_call(
+        kernel,
+        out_shape=jax.ShapeDtypeStruct(shape, jnp.float32),
+        in_specs=[vmem] * len(operands),
+        out_specs=vmem,
+        cost_estimate=pl.CostEstimate(flops=10**6, bytes_accessed=10**7, transcendentals=0),
+    )(*operands)
+
+
+def packed_device(ensemble, obs_cell, obs_value, obs_var, patch_rows):
+    members_dev, lat_rows, lon_cells = ensemble.shape
+    lat_count, member_count = lax.axis_size("lat"), lax.axis_size("member")
+    servers = lat_count * member_count
+    width_cols = lon_cells // servers
+    span = lon_cells // lat_count
+    obs_count = obs_cell.shape[1]
+    patches = patch_rows.shape[1]
+
+    meta = jnp.concatenate(
+        [
+            obs_value,
+            obs_var,
+            obs_cell.astype(jnp.float32),
+            jnp.pad(patch_rows.astype(jnp.float32), ((0, 0), (0, obs_count - patches))),
+        ],
+        axis=0,
+    )
+    near_meta = []
+    for offset in (-1, 0, 1):
+        pairs = []
+        for server in range(servers):
+            member, lat = host_of(server, member_count)
+            pairs.append(((server + offset) % servers, member * lat_count + lat))
+        near_meta.append(lax.ppermute(meta, ("member", "lat"), pairs))
+
+    cells = ensemble.transpose(1, 2, 0)
+    piece = members_dev - LANES
+    rest = cells[:, :, LANES:].transpose(1, 0, 2).reshape(1, lon_cells, lat_rows * piece)
+    packed = jnp.concatenate([cells[:, :, :LANES], rest], axis=0)
+    wide = jnp.concatenate([packed[:, -STEPS:], packed, packed[:, :STEPS]], axis=1)
+    outgoing = jnp.stack(
+        [
+            wide[:, group_of(lat) * span : group_of(lat) * span + span + 2 * STEPS]
+            for lat in range(lat_count)
+        ]
+    )
+    got = exchange(
+        outgoing,
+        lat_count,
+        lambda p: {"lat": p},
+        lambda p: p,
+        lambda p: p,
+        lambda: lax.axis_index("lat"),
+        1,
+    )
+    strips = local(
+        functools.partial(forecast_kernel, member_count, width_cols),
+        (member_count, lat_count, lat_rows + 1, width_cols, LANES),
+        got,
+    )
+    got = exchange(
+        strips,
+        member_count,
+        lambda p: {"member": p},
+        lambda p: turn_of(group_of(lax.axis_index("lat")), p, member_count),
+        lambda p: p,
+        lambda: lax.axis_index("member"),
+        2,
+    )
+    states = local(gather_kernel, (lat_count * lat_rows * width_cols, members_dev * member_count), got)
+    observed = jnp.take(states, near_meta[1][2].astype(jnp.int32), axis=0)
+    before, after = ring(observed, member_count, lat_count, 3)
+    near = jnp.concatenate([before, observed, after], axis=0)
+    near_mean = jnp.mean(near, axis=1)
+    spread = near - near_mean[:, None]
+    joined = jnp.concatenate(near_meta, axis=1)
+    places = joined[2].astype(jnp.int32)
+    shifts = jnp.repeat(jnp.array([-1.0, 0.0, 1.0], jnp.float32), obs_count) * width_cols
+    obs_meta = (
+        joined[0] - near_mean,
+        joined[1],
+        (places // width_cols).astype(jnp.float32),
+        (places % width_cols).astype(jnp.float32) + shifts,
+    )
+    lengths = near_meta[1][3, :patches].astype(jnp.int32)
+    analysed = analyse(states, spread, obs_meta, lengths, width_cols)
+    outgoing = local(
+        functools.partial(scatter_kernel, lat_count, width_cols),
+        (servers, lat_rows + 1, width_cols, LANES),
+        analysed,
+    )
+    got = exchange(
+        outgoing,
+        servers,
+        lambda p: {"member": p // lat_count, "lat": p % lat_count},
+        lambda p: p,
+        lambda p: server_of(p // lat_count, p % lat_count, member_count),
+        lambda: lax.axis_index("member") * lat_count + lax.axis_index("lat"),
+        4,
+    )
+    main = got[:, :lat_rows].transpose(3, 1, 0, 2).reshape(LANES, lat_rows, lon_cells)
+    rest = got[:, lat_rows].reshape(lon_cells, lat_rows, piece).transpose(2, 1, 0)
+    return jnp.concatenate([main, rest], axis=0)
+
+
+def per_device(ensemble, obs_cell, obs_value, obs_var, patch_rows):
+    members_dev, lat_rows, lon_cells = ensemble.shape
+    lat_count, member_count = lax.axis_size("lat"), lax.axis_size("member")
+    fits = (
+        (members_dev - LANES) * lat_rows == LANES
+        and member_count == lat_rows
+        and lat_count % 4 == 0
+        and lon_cells // (lat_count * member_count) == 8
+        and STEPS == 4
+        and patch_rows.shape[1] <= obs_cell.shape[1]
+    )
+    device = packed_device if fits else plain_device
+    return device(ensemble, obs_cell, obs_value, obs_var, patch_rows)
 
 
 def solution(mesh):

time: 165 us -> 153 us (0.927)
  Pallas kernels: 0 us -> 76.7 us
  waiting for transfers between devices: 55.9 us -> 0.01 us
  blocking collectives: 29.2 us -> 0 us
  starting transfers between devices: 23.6 us -> 8.21 us
  other arithmetic: 12.1 us -> 18.9 us
  matrix products: 20.3 us -> 23.8 us
    pallas_call x0 -> x7, Pallas kernels: none -> 76.7 us  [the longest x3 52.2 us: exchange(): pl.pallas_call(functools.partial(exchange_kernel, count, place, source, t...]
    ppermute x6 -> x3, waiting for transfers between devices: 34.7 us -> 0.01 us  [packed_device(): near_meta.append(lax.ppermute(meta, ('member', 'lat'), pairs))]
    all_to_all x1 -> x0, blocking collectives: 29.2 us -> none  [per_device(): lax.all_to_all(outgoing, ('member', 'lat'), split_axis=0, concat_axis=3,...]
    all_to_all x1 -> x0, waiting for transfers between devices: 21.2 us -> none  [per_device(): lax.all_to_all(blocks, ('member', 'lat'), split_axis=3, concat_axis=0, ti...]
    ppermute x6 -> x3, starting transfers between devices: 17 us -> 8.21 us  [packed_device(): near_meta.append(lax.ppermute(meta, ('member', 'lat'), pairs))]
    all_to_all x1 -> x0, starting transfers between devices: 6.62 us -> none  [per_device(): lax.all_to_all(blocks, ('member', 'lat'), split_axis=3, concat_axis=0, ti...]
    unnamed x54 -> x64, local copies, waits for them, and re-layouts: 3.6 us -> 9.36 us
    dot_general x14, matrix products: 16.7 us -> 22.3 us  [dot3(): jnp.matmul(left, right, precision=lax.Precision.HIGH, preferred_element_t...]
  transfers between devices with their start and end apart: 7 -> 3, of which waited for: 4 -> 0; matrix products, arithmetic and copies ran while one was open for 2% -> 3% of each run, Pallas kernels for 0% -> 25%
where the time goes in v1:
time: 153 us; the launch traced here: 152 us
  Pallas kernels  76.7 us (50%)
  matrix products  23.8 us (16%)
  other arithmetic  18.9 us (12%)
  local copies, waits for them, and re-layouts  15.7 us (10%)
  between operations  8.79 us (6%)
  starting transfers between devices  8.21 us (5%)
    pallas_call x3, Pallas kernels, exchange(): pl.pallas_call(functools.partial(exchange_kernel, count, place, source, t...  52.2 us
    dot_general x14, matrix products, dot3(): jnp.matmul(left, right, precision=lax.Precision.HIGH, preferred_element_t...  22.3 us
    pallas_call x1, Pallas kernels, ring(): pl.pallas_call(functools.partial(ring_kernel, member_count, lat_count), o...  14.8 us
    pallas_call x3, Pallas kernels, local(): pl.pallas_call(kernel, out_shape=jax.ShapeDtypeStruct(shape, jnp.float32)...  9.66 us
    unnamed x64, local copies, waits for them, and re-layouts  9.36 us
    ppermute x3, starting transfers between devices, packed_device(): near_meta.append(lax.ppermute(meta, ('member', 'lat'), pairs))  8.21 us
    add x1, other arithmetic, analyse(): high = c1 * x + c2 * x2 + c3 * x3 + c4 * x4  3.23 us
  transfers between devices with their start and end apart: 3, of which 0 were waited for; matrix products, arithmetic and copies ran while one was open for 3% of the time, Pallas kernels for 25%

profile of v1, /device:TPU:0, one launch (start us, length us, event | category | flops | bytes accessed | tf_op | source)
XLA Modules:
  0.0 152.1 jit_solution(17752167133554638506)
XLA Ops:
  1.3 0.7 select_maximum_fusion
  2.7 5.4 %collective-permute-start.1 = (f32[4,128]{1,0:T(4,128)S(1)}, f32[4,128]{1,0:T(4,128)S(1)}, u32[]{:S(2)}, u32[]{:S(2)}) collective-permute-start(f32[4,128]{1,0:T(4,128)S(1)} %select_maximum_fusion), channel_id=1, source_target_pairs={{31,0},{0,8},{1,16},{2,24},{3,25},{4,17},{5,9},{6,1},{7,3},{8,11},... | collective-permute-start | bytes 6152 | tf_op jit(solution)/shard_map/ppermute | solution.py:430
  8.1 2.1 %collective-permute-start.2 = (f32[4,128]{1,0:T(4,128)S(1)}, f32[4,128]{1,0:T(4,128)S(1)}, u32[]{:S(2)}, u32[]{:S(2)}) collective-permute-start(f32[4,128]{1,0:T(4,128)S(1)} %select_maximum_fusion), channel_id=1, source_target_pairs={{1,0},{2,8},{3,16},{4,24},{5,25},{6,17},{7,9},{8,1},{9,3},{10,11},... | collective-permute-start | bytes 6152 | tf_op jit(solution)/shard_map/ppermute | solution.py:430
  10.2 1.4 copy.45
  12.2 0.9 copy-done.20
  13.1 20.1 %shard_map.64.x_ref = f32[8,5,40,128]{3,2,1,0:T(8,128)} custom-call(f32[8,5,40,128]{3,2,1,0:T(8,128)} %copy-done.20), custom_call_target="tpu_custom_call" | custom-call | bytes 32768000 | tf_op jit(solution)/shard_map/pallas_call | solution.py:262
  33.1 5.5 %shard_map.65.x_ref = f32[4,8,5,8,128]{4,3,2,1,0:T(8,128)} custom-call(f32[8,5,40,128]{3,2,1,0:T(8,128)} %shard_map.64.x_ref), custom_call_target="tpu_custom_call" | custom-call | flops 1000000 | bytes 10000000 | tf_op jit(solution)/shard_map/pallas_call | solution.py:397
  38.6 10.4 %shard_map.66.x_ref = f32[4,8,5,8,128]{4,3,2,1,0:T(8,128)} custom-call(f32[4,8,5,8,128]{4,3,2,1,0:T(8,128)} %shard_map.65.x_ref), custom_call_target="tpu_custom_call" | custom-call | bytes 26214400 | tf_op jit(solution)/shard_map/pallas_call | solution.py:262
  49.0 2.1 %shard_map.67 = f32[256,640]{1,0:T(8,128)} custom-call(f32[4,8,5,8,128]{4,3,2,1,0:T(8,128)} %shard_map.66.x_ref), custom_call_target="tpu_custom_call" | custom-call | flops 1000000 | bytes 10000000 | tf_op jit(solution)/shard_map/pallas_call | solution.py:397
  51.1 1.3 reduce_sum.94
  53.0 1.2 broadcast_subtract_fusion
  54.4 0.8 gather_fusion
  55.2 0.8 broadcast_select_fusion.x_ref
  56.0 14.8 %shard_map.68 = (f32[128,640]{1,0:T(8,128)}, f32[128,640]{1,0:T(8,128)}) custom-call(f32[128,640]{1,0:T(8,128)} %broadcast_select_fusion.x_ref), custom_call_target="tpu_custom_call" | custom-call | bytes 8192000 | tf_op jit(solution)/shard_map/pallas_call | solution.py:309
  70.8 1.4 fusion.35
  72.6 0.7 fusion.130
  76.7 0.7 fusion.1
  77.4 0.7 fusion.3
  83.5 1.6 %fusion.4 = f32[384,640]{1,0:T(8,128)S(1)} fusion(f32[384,640]{1,0:T(8,128)S(1)} %fusion.34, f32[256,640]{1,0:T(8,128)S(1)} %broadcast_subtract_fusion), kind=kOutput, calls=%fused_computation.13 | convolution fusion | flops 944128000 | bytes 2621440 | tf_op jit(solution)/shard_map/dot_general | solution.py:60
  85.7 1.2 divide_reduce_fusion.1
  86.8 1.3 divide_reduce_fusion
  88.5 0.7 fusion.132
  89.2 0.8 copy-done.5
  90.0 2.1 %fusion.26 = f32[384,768]{1,0:T(8,128)} fusion(f32[384,384]{1,0:T(8,128)S(1)} %fusion.132, f32[384,384]{1,0:T(8,128)S(1)} %get-tuple-element.35), kind=kOutput, calls=%fused_computation.43 | convolution fusion | flops 679772160 | bytes 2359296 | tf_op jit(solution)/shard_map/dot_general | solution.py:60
  92.1 0.7 fusion.131
  92.9 0.8 copy-done.8
  93.7 2.1 %fusion.18 = f32[384,768]{1,0:T(8,128)} fusion(f32[384,384]{1,0:T(8,128)S(1)} %fusion.131, f32[384,384]{1,0:T(8,128)S(1)} %get-tuple-element.34), kind=kOutput, calls=%fused_computation.35 | convolution fusion | flops 679772160 | bytes 2359296 | tf_op jit(solution)/shard_map/dot_general | solution.py:60
  96.0 3.2 %fusion.36 = (f32[384,384]{1,0:T(8,128)S(1)}, f32[384,384]{1,0:T(8,128)S(1)}, f32[384,384]{1,0:T(8,128)}, f32[384,384]{1,0:T(8,128)S(1)}) fusion(f32[384,768]{1,0:T(8,128)} %fusion.26, f32[384,384]{1,0:T(8,128)} %copy-done.5, f32[384,384]{1,0:T(8,128)S(1)} %get-tuple-element.35, f32[]{:T(128)S(6)} %add.471, f32[]{:T(128)S(6)} %add.474, f32[]{:T(128)S(6)} %add.473, ...), kind=kLoop, calls=%fused_computation.64 | loop fusion | flops 3538944 | bytes 7077912 | tf_op jit(solution)/shard_map/add | solution.py:107
  99.2 1.2 fusion.30
  100.5 0.7 convolution_add_fusion.3
  101.5 0.8 copy-done.6
  102.3 1.5 fusion.17
  103.8 0.8 copy.48
  104.7 2.5 %fusion.22 = f32[768,257]{1,0:T(8,128)S(1)} fusion(f32[384,384]{1,0:T(8,128)S(1)} %get-tuple-element.51, f32[384,384]{1,0:T(8,128)} %get-tuple-element.50, f32[384,1]{1,0:T(8,128)S(1)} %copy.48, f32[384,256]{1,0:T(8,128)S(1)} %get-tuple-element.32), kind=kOutput, calls=%fused_computation.39 | convolution fusion | flops 455147904 | bytes 2363904 | tf_op jit(solution)/shard_map/dot_general | solution.py:60
  107.2 0.7 convolution_add_fusion.6
  108.3 0.8 copy-done.10
  109.1 1.5 fusion.13
  110.6 2.7 %fusion.12 = f32[384,257]{1,0:T(8,128)S(1)} fusion(f32[384,257]{1,0:T(8,128)} %fusion.13, f32[384,384]{1,0:T(8,128)S(1)} %get-tuple-element.51, f32[384,257]{1,0:T(8,128)} %copy-done.10, f32[768,257]{1,0:T(8,128)} %copy-done.13, f32[384,1]{1,0:T(8,128)S(1)} %copy.48, f32[384,256]{1,0:T(8,128)S(1)} %get-tuple-element.32, f32[]{:T(128)S(6)} %mul.745, ...), kind=kOutput, calls=%fused_computation.29 | convolution fusion | flops 229153536 | bytes 5116416 | tf_op jit(solution)/shard_map/dot_general | solution.py:60
  113.3 0.8 copy-done.14
  114.5 0.8 copy-done.7
  115.2 2.3 %fusion.16 = f32[384,257]{1,0:T(8,128)S(1)} fusion(f32[384,257]{1,0:T(8,128)} %fusion.17, f32[384,384]{1,0:T(8,128)S(1)} %get-tuple-element.30, f32[384,257]{1,0:T(8,128)S(1)} %copy-done.7, f32[768,257]{1,0:T(8,128)} %copy-done.12, f32[384,1]{1,0:T(8,128)S(1)} %copy.54, f32[384,256]{1,0:T(8,128)S(1)} %get-tuple-element.33, f32[]{:T(128)S(6)} %mul.815, ...), kind=kOutput, calls=%fused_computation.33 | convolution fusion | flops 229153536 | bytes 4531200 | tf_op jit(solution)/shard_map/dot_general | solution.py:60
  117.6 0.8 copy-done.16
  121.0 2.6 %fusion.108 = (f32[256]{0:T(256)S(1)}, pred[256]{0:T(512)(128)(4,1)S(1)}, pred[256]{0:T(512)(128)(4,1)S(1)}) fusion(f32[256]{0:T(256)S(1)} %add_reduce_fusion, f32[256]{0:T(256)S(1)} %add_reduce_fusion.1, f32[]{:T(128)} %reduce_max.19, f32[]{:T(128)} %reduce_max.18, f32[256]{0:T(256)S(1)} %copy-done.22, s32[]{:T(128)S(6)} %add.422, s32[]{:T(128)} %bitcast.14, ...), kind=kLoop, calls=%fused_computation.223 | loop fusion | flops 5376 | bytes 4632 | tf_op jit(solution)/shard_map/add | solution.py:129
  123.6 1.8 %convolution_add_fusion.x_ref = f32[256,640]{1,0:T(8,128)} fusion(f32[384,640]{1,0:T(8,128)S(1)} %copy-done.2, f32[256,640]{1,0:T(8,128)S(1)} %copy-done.4, f32[384,257]{1,0:T(8,128)S(1)} %copy-done.17, f32[384,257]{1,0:T(8,128)S(1)} %copy-done.15, f32[256]{0:T(256)S(1)} %select_select_fusion, f32[256]{0:T(256)S(1)} %get-tuple-element.12, ...), kind=kOutput, calls=%fused_computation.20 | convolution fusion | flops 378372096 | bytes 3087360 | tf_op jit(solution)/shard_map/dot_general | solution.py:60
  125.5 2.1 %shard_map.69.x_ref = f32[32,5,8,128]{3,2,1,0:T(8,128)} custom-call(f32[256,640]{1,0:T(8,128)} %convolution_add_fusion.x_ref), custom_call_target="tpu_custom_call" | custom-call | flops 1000000 | bytes 10000000 | tf_op jit(solution)/shard_map/pallas_call | solution.py:397
  127.5 21.8 %shard_map.70 = f32[32,5,8,128]{3,2,1,0:T(8,128)} custom-call(f32[32,5,8,128]{3,2,1,0:T(8,128)} %shard_map.69.x_ref), custom_call_target="tpu_custom_call" | custom-call | bytes 26214400 | tf_op jit(solution)/shard_map/pallas_call | solution.py:262
  149.4 1.1 copy_bitcast_fusion.1
  150.9 1.1 copy.62
  (111 shorter events, 9.0 us)
Async XLA Ops:
  2.0 52.3 %collective-permute-start = (f32[4,128]{1,0:T(4,128)S(1)}, f32[4,128]{1,0:T(4,128)S(1)}, u32[]{:S(2)}, u32[]{:S(2)}) collective-permute-start(f32[4,128]{1,0:T(4,128)S(1)} %select_maximum_fusion), channel_id=1, source_target_pairs={{0,0},{1,8},{2,16},{3,24},{4,25},{5,17},{6,9},{7,1},{8,3},{9,11},{... | collective-permute-start | bytes 6152 | tf_op jit(solution)/shard_map/ppermute | solution.py:430
  2.7 51.6 %collective-permute-start.1 = (f32[4,128]{1,0:T(4,128)S(1)}, f32[4,128]{1,0:T(4,128)S(1)}, u32[]{:S(2)}, u32[]{:S(2)}) collective-permute-start(f32[4,128]{1,0:T(4,128)S(1)} %select_maximum_fusion), channel_id=1, source_target_pairs={{31,0},{0,8},{1,16},{2,24},{3,25},{4,17},{5,9},{6,1},{7,3},{8,11},... | collective-permute-start | bytes 6152 | tf_op jit(solution)/shard_map/ppermute | solution.py:430
  8.1 46.2 %collective-permute-start.2 = (f32[4,128]{1,0:T(4,128)S(1)}, f32[4,128]{1,0:T(4,128)S(1)}, u32[]{:S(2)}, u32[]{:S(2)}) collective-permute-start(f32[4,128]{1,0:T(4,128)S(1)} %select_maximum_fusion), channel_id=1, source_target_pairs={{1,0},{2,8},{3,16},{4,24},{5,25},{6,17},{7,9},{8,1},{9,3},{10,11},... | collective-permute-start | bytes 6152 | tf_op jit(solution)/shard_map/ppermute | solution.py:430
  12.2 0.9 copy-start.20
  51.1 3.1 %copy-start.29 = (f32[3]{0:T(128)S(1)}, f32[3]{0:T(128)}, u32[]{:S(2)}) copy-start(f32[3]{0:T(128)} %constant.131) | copy-start | bytes 40
  51.1 3.3 %copy-start = (f32[256,640]{1,0:T(8,128)S(1)}, f32[256,640]{1,0:T(8,128)}, u32[]{:S(2)}) copy-start(f32[256,640]{1,0:T(8,128)} %shard_map.67) | copy-start | bytes 1966084
  52.4 0.6 copy-start.21
  54.2 29.3 %copy-start.3 = (f32[256,640]{1,0:T(8,128)}, f32[256,640]{1,0:T(8,128)S(1)}, u32[]{:S(2)}) copy-start(f32[256,640]{1,0:T(8,128)S(1)} %broadcast_subtract_fusion) | copy-start | bytes 1966084
  56.0 16.2 %copy-start.11 = (f32[128,640]{1,0:T(8,128)S(1)}, f32[128,640]{1,0:T(8,128)}, u32[]{:S(2)}) copy-start(f32[128,640]{1,0:T(8,128)} %broadcast_select_fusion.x_ref) | copy-start | bytes 983044
  70.8 1.4 copy-start.18
  70.8 1.4 copy-start.19
  72.4 11.1 %copy-start.1 = (f32[384,640]{1,0:T(8,128)}, f32[384,640]{1,0:T(8,128)S(1)}, u32[]{:S(2)}) copy-start(f32[384,640]{1,0:T(8,128)S(1)} %fusion.34) | copy-start | bytes 2949124
  76.6 0.8 copy-start.23
  76.6 0.8 copy-start.25
  89.2 0.8 copy-start.5
  92.9 0.8 copy-start.8
  100.5 1.0 copy-start.12
  101.5 0.8 copy-start.6
  107.2 1.1 copy-start.13
  107.2 1.9 %copy-start.9 = (f32[384,384]{1,0:T(8,128)S(1)}, f32[384,384]{1,0:T(8,128)}, u32[]{:S(2)}) copy-start(f32[384,384]{1,0:T(8,128)} %get-tuple-element.50) | copy-start | bytes 1769476
  108.3 0.8 copy-start.10
  113.3 0.8 copy-start.14
  114.1 1.1 copy-start.7
  115.2 4.9 %copy-start.27 = (f32[1,384]{1,0:T(1,128)S(1)}, f32[1,384]{1,0:T(1,128)}, u32[]{:S(2)}) copy-start(f32[1,384]{1,0:T(1,128)} %get-tuple-element.21) | copy-start | bytes 4612
  115.2 4.9 %copy-start.28 = (f32[1,384]{1,0:T(1,128)S(1)}, f32[1,384]{1,0:T(1,128)}, u32[]{:S(2)}) copy-start(f32[1,384]{1,0:T(1,128)} %get-tuple-element.27) | copy-start | bytes 4612
  117.6 0.8 copy-start.16
  118.4 2.1 %copy-start.24 = (f32[384]{0:T(512)S(1)}, f32[384]{0:T(512)}, u32[]{:S(2)}) copy-start(f32[384]{0:T(512)} %copy-done.23) | copy-start | bytes 4612
  118.4 2.1 %copy-start.26 = (f32[384]{0:T(512)S(1)}, f32[384]{0:T(512)}, u32[]{:S(2)}) copy-start(f32[384]{0:T(512)} %copy-done.25) | copy-start | bytes 4612
  118.5 2.0 %copy-start.17 = (f32[384,257]{1,0:T(8,128)S(1)}, f32[384,257]{1,0:T(8,128)}, u32[]{:S(2)}) copy-start(f32[384,257]{1,0:T(8,128)} %copy-done.16) | copy-start | bytes 1184260
  118.5 2.2 %copy-start.15 = (f32[384,257]{1,0:T(8,128)S(1)}, f32[384,257]{1,0:T(8,128)}, u32[]{:S(2)}) copy-start(f32[384,257]{1,0:T(8,128)} %copy-done.14) | copy-start | bytes 1184260
  120.3 0.7 copy-start.22
  120.3 3.3 %copy-start.2 = (f32[384,640]{1,0:T(8,128)S(1)}, f32[384,640]{1,0:T(8,128)}, u32[]{:S(2)}) copy-start(f32[384,640]{1,0:T(8,128)} %copy-done.1) | copy-start | bytes 2949124
  120.3 3.3 %copy-start.4 = (f32[256,640]{1,0:T(8,128)S(1)}, f32[256,640]{1,0:T(8,128)}, u32[]{:S(2)}) copy-start(f32[256,640]{1,0:T(8,128)} %copy-done.3) | copy-start | bytes 1966084
  149.4 1.1 slice-start

commit v2 on v1

--- a/solution.py
+++ b/solution.py
@@ -190,22 +190,27 @@
 LANES = 128
 
 
-def group_of(place):
-    return place + (place % 4) // 2 * (1 - 2 * (place % 2))
+def group_of(place, size):
+    return place % 2 * (size - 1 - place // 2) + (1 - place % 2) * (place // 2)
+
+
+def place_of(group, size):
+    late = group * 2 // size
+    return late * (2 * (size - 1 - group) + 1) + (1 - late) * 2 * group
 
 
 def turn_of(group, index, size):
     return (group % 2) * (size - 1 - index) + (1 - group % 2) * index
 
 
-def server_of(member, lat, member_count):
-    group = group_of(lat)
+def server_of(member, lat, member_count, lat_count):
+    group = group_of(lat, lat_count)
     return member_count * group + turn_of(group, member, member_count)
 
 
-def host_of(server, member_count):
+def host_of(server, member_count, lat_count):
     group = server // member_count
-    return turn_of(group, server % member_count, member_count), group_of(group)
+    return turn_of(group, server % member_count, member_count), place_of(group, lat_count)
 
 
 def exchange_kernel(count, place, source, target, me_of, x_ref, o_ref, send_sem, recv_sem, own_sem):
@@ -276,10 +281,10 @@
 
 def ring_kernel(member_count, lat_count, x_ref, before_ref, after_ref, send_sem, recv_sem):
     servers = member_count * lat_count
-    me = server_of(lax.axis_index("member"), lax.axis_index("lat"), member_count)
+    me = server_of(lax.axis_index("member"), lax.axis_index("lat"), member_count, lat_count)
 
     def place(server):
-        member, lat = host_of(server, member_count)
+        member, lat = host_of(server, member_count, lat_count)
         return {"member": member, "lat": lat}
 
     up, down = place(lax.rem(me + 1, servers)), place(lax.rem(me + servers - 1, servers))
@@ -392,6 +397,90 @@
         o_ref[own, lat_rows] = total
 
 
+def halves(value):
+    high = value.astype(jnp.bfloat16)
+    return high, (value - high.astype(jnp.float32)).astype(jnp.bfloat16)
+
+
+def dot_halves(left, right, turned=False):
+    dims = (((1,), (1 if turned else 0,)), ((), ()))
+    dot = functools.partial(lax.dot_general, dimension_numbers=dims, preferred_element_type=jnp.float32)
+    return dot(left[0], right[0]) + (dot(left[0], right[1]) + dot(left[1], right[0]))
+
+
+def solve_kernel(
+    states_ref, before_ref, own_ref, after_ref, value_ref, row_ref, col_ref, mask_ref, o_ref
+):
+    cells, members = states_ref.shape
+    patches = row_ref.shape[0]
+    states = states_ref[...]
+    state_mean = jnp.mean(states, axis=1, keepdims=True)
+    anomaly = states - state_mean
+    near = jnp.concatenate([before_ref[...], own_ref[...], after_ref[...]], axis=0)
+    spread = near - jnp.mean(near, axis=1, keepdims=True)
+    count = near.shape[0]
+    near_halves = halves(near)
+    ones = jnp.ones((8, members), jnp.bfloat16)
+    sums = sum(
+        lax.dot_general(ones, part, (((1,), (1,)), ((), ())), preferred_element_type=jnp.float32)
+        for part in near_halves
+    )
+    innov = value_ref[...] - sums * (1.0 / members)
+    spread_halves, anomaly_halves = halves(spread), halves(anomaly)
+    common = dot_halves(spread_halves, spread_halves, True)
+    crossed = dot_halves(anomaly_halves, spread_halves, True)
+    turned = spread.T
+    degrees = members - 1.0
+    shift, shrink = state_mean, jnp.zeros((cells, 1), jnp.float32)
+    weights_all = jnp.zeros((cells, count), jnp.float32)
+    for patch in range(patches):
+        row, col, mask = row_ref[patch], col_ref[patch], mask_ref[patch]
+        outer = jnp.dot(
+            (turned * (row * row)).astype(jnp.bfloat16),
+            spread_halves[0],
+            preferred_element_type=jnp.float32,
+        )
+        bound = degrees + jnp.max(jnp.sum(jnp.abs(outer), axis=0, keepdims=True), axis=1, keepdims=True)
+        inverse = 1.0 / bound
+        alpha = degrees * inverse
+        x = common * col * (row * inverse)
+        c0 = 2.25 + alpha * (-2.4375 + alpha * (1.6875 + alpha * (-0.5625 + alpha * 0.0625)))
+        c1 = -2.4375 + alpha * (3.375 + alpha * (-1.6875 + alpha * 0.25))
+        c2 = 1.6875 + alpha * (-1.6875 + alpha * 0.375)
+        c3 = -0.5625 + alpha * 0.25
+        c4 = 0.0625
+        x_halves = halves(x)
+        x2 = dot_halves(x_halves, x_halves)
+        x2_halves = halves(x2)
+        x3 = dot_halves(x2_halves, x_halves)
+        x4 = dot_halves(x2_halves, x2_halves)
+        low = halves(c2 * x + c3 * x2 + c4 * x3)
+        high = halves(c1 * x + c2 * x2 + c3 * x3 + c4 * x4)
+        block = jnp.concatenate([crossed, innov], axis=0) * row
+        block_halves = halves(block)
+        b1 = c1 * block + dot_halves(block_halves, low)
+        b2 = c0 * block + dot_halves(block_halves, high)
+        b3 = c0 * b2 + dot_halves(halves(b2), high)
+        mixed = alpha * c0 * b1 + b3
+        got = 1.5 * b1 - 0.5 * (
+            alpha * c0 * c0 * b1
+            + c0 * mixed
+            + dot_halves(halves(mixed), high)
+            + alpha * (c1 * b3 + dot_halves(halves(b3), low))
+        )
+        base = c0 * (1.5 - 0.5 * alpha * c0 * c0)
+        driven = base * block[cells:] + dot_halves(halves(got[cells:]), x_halves)
+        again = dot_halves(halves(driven), x_halves)
+        mean_part = inverse * jnp.sum(
+            block[:cells] * (base * driven[:1]) + got[:cells] * again[:1], axis=1, keepdims=True
+        )
+        root_scale = jnp.sqrt(alpha)
+        shift = shift + mask * mean_part
+        shrink = shrink + mask * (root_scale * base)
+        weights_all = weights_all + mask * (got[:cells] * (row * (root_scale * inverse)))
+    o_ref[...] = shift + shrink * anomaly + dot_halves(halves(weights_all), spread_halves)
+
+
 def local(kernel, shape, *operands):
     vmem = pl.BlockSpec(memory_space=pltpu.VMEM)
     return pl.pallas_call(
@@ -425,7 +514,7 @@
     for offset in (-1, 0, 1):
         pairs = []
         for server in range(servers):
-            member, lat = host_of(server, member_count)
+            member, lat = host_of(server, member_count, lat_count)
             pairs.append(((server + offset) % servers, member * lat_count + lat))
         near_meta.append(lax.ppermute(meta, ("member", "lat"), pairs))
 
@@ -436,7 +525,7 @@
     wide = jnp.concatenate([packed[:, -STEPS:], packed, packed[:, :STEPS]], axis=1)
     outgoing = jnp.stack(
         [
-            wide[:, group_of(lat) * span : group_of(lat) * span + span + 2 * STEPS]
+            wide[:, group_of(lat, lat_count) * span : group_of(lat, lat_count) * span + span + 2 * STEPS]
             for lat in range(lat_count)
         ]
     )
@@ -458,7 +547,7 @@
         strips,
         member_count,
         lambda p: {"member": p},
-        lambda p: turn_of(group_of(lax.axis_index("lat")), p, member_count),
+        lambda p: turn_of(group_of(lax.axis_index("lat"), lat_count), p, member_count),
         lambda p: p,
         lambda: lax.axis_index("member"),
         2,
@@ -466,20 +555,38 @@
     states = local(gather_kernel, (lat_count * lat_rows * width_cols, members_dev * member_count), got)
     observed = jnp.take(states, near_meta[1][2].astype(jnp.int32), axis=0)
     before, after = ring(observed, member_count, lat_count, 3)
-    near = jnp.concatenate([before, observed, after], axis=0)
-    near_mean = jnp.mean(near, axis=1)
-    spread = near - near_mean[:, None]
     joined = jnp.concatenate(near_meta, axis=1)
     places = joined[2].astype(jnp.int32)
     shifts = jnp.repeat(jnp.array([-1.0, 0.0, 1.0], jnp.float32), obs_count) * width_cols
-    obs_meta = (
-        joined[0] - near_mean,
-        joined[1],
-        (places // width_cols).astype(jnp.float32),
-        (places % width_cols).astype(jnp.float32) + shifts,
-    )
     lengths = near_meta[1][3, :patches].astype(jnp.int32)
-    analysed = analyse(states, spread, obs_meta, lengths, width_cols)
+    starts = jnp.cumsum(lengths) - lengths
+    lat_total = lat_count * lat_rows
+    scale = jnp.sqrt(
+        localize(
+            (places // width_cols).astype(jnp.float32)[None],
+            ((places % width_cols).astype(jnp.float32) + shifts)[None],
+            starts[:, None],
+            lengths[:, None],
+            lat_total / 4.0,
+            float(width_cols),
+        )
+        / joined[1][None]
+    )
+    cell_rows = (jnp.arange(lat_total * width_cols, dtype=jnp.int32) // width_cols)[None, :, None]
+    begins = starts[:, None, None]
+    mask = ((cell_rows >= begins) & (cell_rows < begins + lengths[:, None, None])).astype(jnp.float32)
+    analysed = local(
+        solve_kernel,
+        states.shape,
+        states,
+        before,
+        observed,
+        after,
+        joined[:1],
+        scale[:, None, :],
+        scale[:, :, None],
+        mask,
+    )
     outgoing = local(
         functools.partial(scatter_kernel, lat_count, width_cols),
         (servers, lat_rows + 1, width_cols, LANES),
@@ -490,7 +597,7 @@
         servers,
         lambda p: {"member": p // lat_count, "lat": p % lat_count},
         lambda p: p,
-        lambda p: server_of(p // lat_count, p % lat_count, member_count),
+        lambda p: server_of(p // lat_count, p % lat_count, member_count, lat_count),
         lambda: lax.axis_index("member") * lat_count + lax.axis_index("lat"),
         4,
     )
@@ -505,7 +612,7 @@
     fits = (
         (members_dev - LANES) * lat_rows == LANES
         and member_count == lat_rows
-        and lat_count % 4 == 0
+        and lat_count % 2 == 0
         and lon_cells // (lat_count * member_count) == 8
         and STEPS == 4
         and patch_rows.shape[1] <= obs_cell.shape[1]

time: 153 us -> 115 us (0.75)
  matrix products: 23.8 us -> 0 us
  other arithmetic: 18.9 us -> 5.03 us
  Pallas kernels: 76.7 us -> 89.8 us
  between operations: 8.79 us -> 0.25 us
  local copies, waits for them, and re-layouts: 15.7 us -> 8.53 us
  starting transfers between devices: 8.21 us -> 10.9 us
    dot_general x16 -> x0, matrix products: 23.8 us -> none  [the longest x14 22.3 us: dot3(): jnp.matmul(left, right, precision=lax.Precision.HIGH, preferred_element_t...]
    pallas_call x3 -> x4, Pallas kernels: 9.66 us -> 25.7 us  [local(): pl.pallas_call(kernel, out_shape=jax.ShapeDtypeStruct(shape, jnp.float32)...]
    add x3 -> x0, other arithmetic: 5.85 us -> none  [the longest x1 3.23 us: analyse(): high = c1 * x + c2 * x2 + c3 * x3 + c4 * x4]
    unnamed x64 -> x14, local copies, waits for them, and re-layouts: 9.36 us -> 3.62 us
    reduce_sum x8 -> x0, other arithmetic: 3.61 us -> none  [the longest x1 1.38 us: packed_device(): near_mean = jnp.mean(near, axis=1)]
    pallas_call x1, Pallas kernels: 14.8 us -> 11.6 us  [ring(): pl.pallas_call(functools.partial(ring_kernel, member_count, lat_count), o...]
    ppermute x3, starting transfers between devices: 8.21 us -> 10.9 us  [packed_device(): near_meta.append(lax.ppermute(meta, ('member', 'lat'), pairs))]
    div x4 -> x0, other arithmetic: 2.49 us -> none  [the longest x2 2.48 us: analyse(): x = common * scale[:, None] * (scale / bound)[None, :]]
  transfers between devices with their start and end apart: 3 -> 3, of which waited for: 0 -> 0; matrix products, arithmetic and copies ran while one was open for 3% -> 2% of each run, Pallas kernels for 25% -> 32%
where the time goes in v2:
time: 115 us
  Pallas kernels  89.8 us (78%)
  starting transfers between devices  10.9 us (9%)
  local copies, waits for them, and re-layouts  8.53 us (7%)
  other arithmetic  5.03 us (4%)
    pallas_call x3, Pallas kernels, exchange(): pl.pallas_call(functools.partial(exchange_kernel, count, place, source, t...  52.5 us
    pallas_call x4, Pallas kernels, local(): pl.pallas_call(kernel, out_shape=jax.ShapeDtypeStruct(shape, jnp.float32)...  25.7 us
    pallas_call x1, Pallas kernels, ring(): pl.pallas_call(functools.partial(ring_kernel, member_count, lat_count), o...  11.6 us
    ppermute x3, starting transfers between devices, packed_device(): near_meta.append(lax.ppermute(meta, ('member', 'lat'), pairs))  10.9 us
    unnamed x14, local copies, waits for them, and re-layouts  3.62 us
  transfers between devices with their start and end apart: 3, of which 0 were waited for; matrix products, arithmetic and copies ran while one was open for 2% of the time, Pallas kernels for 32%

profile of v2, /device:TPU:0, one launch (start us, length us, event | category | flops | bytes accessed | tf_op | source)
XLA Modules:
  0.0 114.5 jit_solution(8995405828225609607)
XLA Ops:
  0.0 0.0 copy-start.4
  0.0 0.7 convert_element_type.90
  0.7 0.0 copy-done.4
  0.7 0.0 copy-start.2
  0.7 0.0 copy-start.3
  0.7 0.6 copy-done.2
  1.3 0.0 copy-done.3
  1.4 0.7 collective-permute-start
  2.0 5.5 %collective-permute-start.1 = (f32[4,128]{1,0:T(4,128)S(1)}, f32[4,128]{1,0:T(4,128)S(1)}, u32[]{:S(2)}, u32[]{:S(2)}) collective-permute-start(f32[4,128]{1,0:T(4,128)S(1)} %select_maximum_fusion), channel_id=1, source_target_pairs={{31,0},{0,8},{1,16},{2,24},{3,26},{4,18},{5,10},{6,2},{7,4},{8,12}... | collective-permute-start | bytes 6152 | tf_op jit(solution)/shard_map/ppermute | solution.py:519
  7.5 4.8 %collective-permute-start.2 = (f32[4,128]{1,0:T(4,128)S(1)}, f32[4,128]{1,0:T(4,128)S(1)}, u32[]{:S(2)}, u32[]{:S(2)}) collective-permute-start(f32[4,128]{1,0:T(4,128)S(1)} %select_maximum_fusion), channel_id=1, source_target_pairs={{1,0},{2,8},{3,16},{4,24},{5,26},{6,18},{7,10},{8,2},{9,4},{10,12}... | collective-permute-start | bytes 6152 | tf_op jit(solution)/shard_map/ppermute | solution.py:519
  12.3 1.4 %copy.16 = f32[160,4,256]{0,2,1:T(8,128)S(1)} copy(f32[160,4,256]{2,1,0:T(4,128)} %param.6) | data formatting | bytes 1310720 | tf_op args[0]
  13.8 0.2 copy.17
  14.0 0.1 copy.18
  14.2 0.0 copy-start.1
  14.2 0.6 copy-done.1
  14.9 0.0 copy-start
  14.9 0.1 broadcast_bitcast_fusion
  14.9 0.8 copy-done
  15.8 18.6 %shard_map.64.x_ref = f32[8,5,40,128]{3,2,1,0:T(8,128)} custom-call(f32[8,5,40,128]{3,2,1,0:T(8,128)} %copy-done), custom_call_target="tpu_custom_call" | custom-call | bytes 32768000 | tf_op jit(solution)/shard_map/pallas_call | solution.py:267
  34.4 5.5 %shard_map.65.x_ref = f32[4,8,5,8,128]{4,3,2,1,0:T(8,128)} custom-call(f32[8,5,40,128]{3,2,1,0:T(8,128)} %shard_map.64.x_ref), custom_call_target="tpu_custom_call" | custom-call | flops 1000000 | bytes 10000000 | tf_op jit(solution)/shard_map/pallas_call | solution.py:486
  39.9 9.9 %shard_map.66.x_ref = f32[4,8,5,8,128]{4,3,2,1,0:T(8,128)} custom-call(f32[4,8,5,8,128]{4,3,2,1,0:T(8,128)} %shard_map.65.x_ref), custom_call_target="tpu_custom_call" | custom-call | bytes 26214400 | tf_op jit(solution)/shard_map/pallas_call | solution.py:267
  49.8 2.1 %shard_map.67.states_ref = f32[256,640]{1,0:T(8,128)} custom-call(f32[4,8,5,8,128]{4,3,2,1,0:T(8,128)} %shard_map.66.x_ref), custom_call_target="tpu_custom_call" | custom-call | flops 1000000 | bytes 10000000 | tf_op jit(solution)/shard_map/pallas_call | solution.py:486
  51.9 0.0 collective-permute-done
  51.9 0.2 reduce-window.7
  52.1 0.0 collective-permute-done.1
  52.1 0.0 collective-permute-done.2
  52.2 0.5 convert_reduce_fusion
  52.7 1.1 fusion.3.col_ref
  53.8 0.7 fusion.20.row_ref
  54.5 2.0 %gather_fusion = f32[128,640]{1,0:T(8,128)S(1)} fusion(f32[256,640]{1,0:T(8,128)} %shard_map.67.states_ref, s32[1024]{0:T(1024)S(1)} %pad_clamp_fusion), kind=kCustom, calls=%fused_computation | custom fusion | bytes 655872 | tf_op jit(solution)/shard_map/jit(_take)/gather | solution.py:556
  56.5 0.8 broadcast_select_fusion.x_ref.own_ref
  57.3 11.6 %shard_map.68 = (f32[128,640]{1,0:T(8,128)}, f32[128,640]{1,0:T(8,128)}) custom-call(f32[128,640]{1,0:T(8,128)} %broadcast_select_fusion.x_ref.own_ref), custom_call_target="tpu_custom_call" | custom-call | bytes 8192000 | tf_op jit(solution)/shard_map/pallas_call | solution.py:314
  68.9 0.8 and_convert_fusion.mask_ref
  69.8 16.0 %shard_map.69.x_ref = f32[256,640]{1,0:T(8,128)} custom-call(f32[256,640]{1,0:T(8,128)} %shard_map.67.states_ref, f32[128,640]{1,0:T(8,128)} %get-tuple-element.7.before_ref, f32[128,640]{1,0:T(8,128)} %broadcast_select_fusion.x_ref.own_ref, f32[128,640]{1,0:T(8,128)} %get-tuple-element.8.after_ref, f32[1,384]{1,0:T(1,128)} %get-tuple-element.14.value_ref, ...), custom_call_target="tpu_custom_call" | custom-call | flops 1000000 | bytes 10000000 | tf_op jit(solution)/shard_map/pallas_call | solution.py:486
  85.8 2.1 %shard_map.70.x_ref = f32[32,5,8,128]{3,2,1,0:T(8,128)} custom-call(f32[256,640]{1,0:T(8,128)} %shard_map.69.x_ref), custom_call_target="tpu_custom_call" | custom-call | flops 1000000 | bytes 10000000 | tf_op jit(solution)/shard_map/pallas_call | solution.py:486
  87.9 24.0 %shard_map.71 = f32[32,5,8,128]{3,2,1,0:T(8,128)} custom-call(f32[32,5,8,128]{3,2,1,0:T(8,128)} %shard_map.70.x_ref), custom_call_target="tpu_custom_call" | custom-call | bytes 26214400 | tf_op jit(solution)/shard_map/pallas_call | solution.py:267
  111.8 0.0 slice-start
  111.8 1.1 copy_bitcast_fusion.1
  113.0 0.0 slice-done
  113.0 0.3 reshape_squeeze.3
  113.3 0.1 pad_maximum_fusion
  113.4 1.1 %copy.25 = f32[160,4,256]{2,1,0:T(4,128)} copy(f32[160,4,256]{0,2,1:T(8,128)S(1)} %pad_maximum_fusion) | data formatting | bytes 1310720 | tf_op jit(solution)/shard_map/concatenate | solution.py:606
  (23 shorter events, 0.3 us)
Async XLA Ops:
  0.0 0.7 copy-start.4
  0.7 0.7 copy-start.2
  0.7 0.7 copy-start.3
  1.4 50.6 %collective-permute-start = (f32[4,128]{1,0:T(4,128)S(1)}, f32[4,128]{1,0:T(4,128)S(1)}, u32[]{:S(2)}, u32[]{:S(2)}) collective-permute-start(f32[4,128]{1,0:T(4,128)S(1)} %select_maximum_fusion), channel_id=1, source_target_pairs={{0,0},{1,8},{2,16},{3,24},{4,26},{5,18},{6,10},{7,2},{8,4},{9,12},... | collective-permute-start | bytes 6152 | tf_op jit(solution)/shard_map/ppermute | solution.py:519
  2.0 50.1 %collective-permute-start.1 = (f32[4,128]{1,0:T(4,128)S(1)}, f32[4,128]{1,0:T(4,128)S(1)}, u32[]{:S(2)}, u32[]{:S(2)}) collective-permute-start(f32[4,128]{1,0:T(4,128)S(1)} %select_maximum_fusion), channel_id=1, source_target_pairs={{31,0},{0,8},{1,16},{2,24},{3,26},{4,18},{5,10},{6,2},{7,4},{8,12}... | collective-permute-start | bytes 6152 | tf_op jit(solution)/shard_map/ppermute | solution.py:519
  7.5 44.6 %collective-permute-start.2 = (f32[4,128]{1,0:T(4,128)S(1)}, f32[4,128]{1,0:T(4,128)S(1)}, u32[]{:S(2)}, u32[]{:S(2)}) collective-permute-start(f32[4,128]{1,0:T(4,128)S(1)} %select_maximum_fusion), channel_id=1, source_target_pairs={{1,0},{2,8},{3,16},{4,24},{5,26},{6,18},{7,10},{8,2},{9,4},{10,12}... | collective-permute-start | bytes 6152 | tf_op jit(solution)/shard_map/ppermute | solution.py:519
  14.2 0.7 copy-start.1
  14.9 0.9 copy-start
  111.8 1.1 slice-start

commit v3 on v2

--- a/solution.py
+++ b/solution.py
@@ -416,7 +416,8 @@
     states = states_ref[...]
     state_mean = jnp.mean(states, axis=1, keepdims=True)
     anomaly = states - state_mean
-    near = jnp.concatenate([before_ref[...], own_ref[...], after_ref[...]], axis=0)
+    each = value_ref.shape[1] // 3
+    near = jnp.concatenate([before_ref[:each], own_ref[:each], after_ref[:each]], axis=0)
     spread = near - jnp.mean(near, axis=1, keepdims=True)
     count = near.shape[0]
     near_halves = halves(near)
@@ -510,13 +511,11 @@
         ],
         axis=0,
     )
-    near_meta = []
-    for offset in (-1, 0, 1):
-        pairs = []
-        for server in range(servers):
-            member, lat = host_of(server, member_count, lat_count)
-            pairs.append(((server + offset) % servers, member * lat_count + lat))
-        near_meta.append(lax.ppermute(meta, ("member", "lat"), pairs))
+    pairs = []
+    for server in range(servers):
+        member, lat = host_of(server, member_count, lat_count)
+        pairs.append((server, member * lat_count + lat))
+    own_meta = lax.ppermute(meta, ("member", "lat"), pairs)
 
     cells = ensemble.transpose(1, 2, 0)
     piece = members_dev - LANES
@@ -553,12 +552,16 @@
         2,
     )
     states = local(gather_kernel, (lat_count * lat_rows * width_cols, members_dev * member_count), got)
-    observed = jnp.take(states, near_meta[1][2].astype(jnp.int32), axis=0)
+    observed = jnp.take(states, own_meta[2].astype(jnp.int32), axis=0)
+    noted = jnp.pad(own_meta, ((0, 4), (0, states.shape[1] - obs_count)))
+    observed = jnp.concatenate([observed, noted], axis=0)
     before, after = ring(observed, member_count, lat_count, 3)
+    noted = slice(obs_count, obs_count + 4)
+    near_meta = (before[noted, :obs_count], own_meta, after[noted, :obs_count])
     joined = jnp.concatenate(near_meta, axis=1)
     places = joined[2].astype(jnp.int32)
     shifts = jnp.repeat(jnp.array([-1.0, 0.0, 1.0], jnp.float32), obs_count) * width_cols
-    lengths = near_meta[1][3, :patches].astype(jnp.int32)
+    lengths = own_meta[3, :patches].astype(jnp.int32)
     starts = jnp.cumsum(lengths) - lengths
     lat_total = lat_count * lat_rows
     scale = jnp.sqrt(

time: 115 us -> 112 us (0.974)
  starting transfers between devices: 10.9 us -> 0.66 us
  Pallas kernels: 89.8 us -> 95.5 us
  local copies, waits for them, and re-layouts: 8.53 us -> 9.9 us
    ppermute x3 -> x1, starting transfers between devices: 10.9 us -> 0.66 us  [packed_device(): own_meta = lax.ppermute(meta, ('member', 'lat'), pairs)]
    pallas_call x3, Pallas kernels: 52.5 us -> 59.2 us  [exchange(): pl.pallas_call(functools.partial(exchange_kernel, count, place, source, t...]
    slice x0 -> x2, local copies, waits for them, and re-layouts: none -> 1.34 us  [packed_device(): near_meta = (before[noted, :obs_count], own_meta, after[noted, :obs_count])]
    unnamed x14 -> x12, local copies, waits for them, and re-layouts: 3.62 us -> 3.65 us
  transfers between devices with their start and end apart: 3 -> 1, of which waited for: 0 -> 0; matrix products, arithmetic and copies ran while one was open for 2% -> 2% of each run, Pallas kernels for 32% -> 38%
where the time goes in v3:
time: 112 us; the launch traced here: 111 us
  Pallas kernels  95.5 us (85%)
  local copies, waits for them, and re-layouts  9.9 us (9%)
  other arithmetic  5.12 us (5%)
    pallas_call x3, Pallas kernels, exchange(): pl.pallas_call(functools.partial(exchange_kernel, count, place, source, t...  59.2 us
    pallas_call x4, Pallas kernels, local(): pl.pallas_call(kernel, out_shape=jax.ShapeDtypeStruct(shape, jnp.float32)...  25.7 us
    pallas_call x1, Pallas kernels, ring(): pl.pallas_call(functools.partial(ring_kernel, member_count, lat_count), o...  10.6 us
    unnamed x12, local copies, waits for them, and re-layouts  3.65 us
  transfers between devices with their start and end apart: 1, of which 0 were waited for; matrix products, arithmetic and copies ran while one was open for 2% of the time, Pallas kernels for 38%

profile of v3, /device:TPU:0, one launch (start us, length us, event | category | flops | bytes accessed | tf_op | source)
XLA Modules:
  0.0 111.4 jit_solution(17797269874220850581)
XLA Ops:
  0.0 0.0 copy-start.4
  0.0 0.7 convert_element_type.92
  0.7 0.0 copy-done.4
  0.7 0.0 copy-start.2
  0.7 0.0 copy-start.3
  0.7 0.6 copy-done.2
  1.3 0.0 copy-done.3
  1.4 0.7 collective-permute-start
  2.0 1.4 %copy.16 = f32[160,4,256]{0,2,1:T(8,128)S(1)} copy(f32[160,4,256]{2,1,0:T(4,128)} %param.6) | data formatting | bytes 1310720 | tf_op args[0]
  3.5 0.0 copy-start.1
  3.6 0.6 copy-done.1
  4.2 0.1 broadcast_bitcast_fusion
  4.2 0.2 copy.17
  4.4 0.1 copy.18
  4.7 0.0 copy-start
  4.7 0.9 copy-done
  5.6 23.8 %shard_map.64.x_ref = f32[8,5,40,128]{3,2,1,0:T(8,128)} custom-call(f32[8,5,40,128]{3,2,1,0:T(8,128)} %copy-done), custom_call_target="tpu_custom_call" | custom-call | bytes 32768000 | tf_op jit(solution)/shard_map/pallas_call | solution.py:267
  29.4 5.5 %shard_map.65.x_ref = f32[4,8,5,8,128]{4,3,2,1,0:T(8,128)} custom-call(f32[8,5,40,128]{3,2,1,0:T(8,128)} %shard_map.64.x_ref), custom_call_target="tpu_custom_call" | custom-call | flops 1000000 | bytes 10000000 | tf_op jit(solution)/shard_map/pallas_call | solution.py:487
  34.9 11.2 %shard_map.66.x_ref = f32[4,8,5,8,128]{4,3,2,1,0:T(8,128)} custom-call(f32[4,8,5,8,128]{4,3,2,1,0:T(8,128)} %shard_map.65.x_ref), custom_call_target="tpu_custom_call" | custom-call | bytes 26214400 | tf_op jit(solution)/shard_map/pallas_call | solution.py:267
  46.1 2.1 %shard_map.67.states_ref = f32[256,640]{1,0:T(8,128)} custom-call(f32[4,8,5,8,128]{4,3,2,1,0:T(8,128)} %shard_map.66.x_ref), custom_call_target="tpu_custom_call" | custom-call | flops 1000000 | bytes 10000000 | tf_op jit(solution)/shard_map/pallas_call | solution.py:487
  48.2 0.0 collective-permute-done
  48.2 0.2 reduce-window.7
  48.4 2.0 %gather_fusion = f32[128,640]{1,0:T(8,128)S(1)} fusion(f32[256,640]{1,0:T(8,128)} %shard_map.67.states_ref, s32[1024]{0:T(1024)S(1)} %pad_clamp_fusion), kind=kCustom, calls=%fused_computation | custom fusion | bytes 655872 | tf_op jit(solution)/shard_map/jit(_take)/gather | solution.py:555
  50.5 0.1 broadcast_select_fusion
  50.6 0.8 select_maximum_fusion.x_ref.own_ref
  51.3 10.6 %shard_map.68 = (f32[136,640]{1,0:T(8,128)}, f32[136,640]{1,0:T(8,128)}) custom-call(f32[136,640]{1,0:T(8,128)} %select_maximum_fusion.x_ref.own_ref), custom_call_target="tpu_custom_call" | custom-call | bytes 8704000 | tf_op jit(solution)/shard_map/pallas_call | solution.py:314
  61.9 0.7 slice.80
  62.6 0.7 slice.81
  63.3 0.6 maximum_convert_fusion
  63.9 0.7 fusion.20.row_ref
  64.6 1.1 fusion.3.col_ref
  65.6 0.8 and_convert_fusion.mask_ref
  66.5 16.0 %shard_map.69.x_ref = f32[256,640]{1,0:T(8,128)} custom-call(f32[256,640]{1,0:T(8,128)} %shard_map.67.states_ref, f32[136,640]{1,0:T(8,128)} %get-tuple-element.7.before_ref, f32[136,640]{1,0:T(8,128)} %select_maximum_fusion.x_ref.own_ref, f32[136,640]{1,0:T(8,128)} %get-tuple-element.8.after_ref, f32[1,384]{1,0:T(1,128)} %get-tuple-element.14.value_ref, ...), custom_call_target="tpu_custom_call" | custom-call | flops 1000000 | bytes 10000000 | tf_op jit(solution)/shard_map/pallas_call | solution.py:487
  82.5 2.1 %shard_map.70.x_ref = f32[32,5,8,128]{3,2,1,0:T(8,128)} custom-call(f32[256,640]{1,0:T(8,128)} %shard_map.69.x_ref), custom_call_target="tpu_custom_call" | custom-call | flops 1000000 | bytes 10000000 | tf_op jit(solution)/shard_map/pallas_call | solution.py:487
  84.6 24.1 %shard_map.71 = f32[32,5,8,128]{3,2,1,0:T(8,128)} custom-call(f32[32,5,8,128]{3,2,1,0:T(8,128)} %shard_map.70.x_ref), custom_call_target="tpu_custom_call" | custom-call | bytes 26214400 | tf_op jit(solution)/shard_map/pallas_call | solution.py:267
  108.7 0.0 slice-start
  108.7 1.1 %copy_bitcast_fusion.1 = f32[128,4,256]{0,2,1:T(8,128)S(1)} fusion(f32[32,5,8,128]{3,2,1,0:T(8,128)} %shard_map.71), kind=kLoop, calls=%fused_computation.5 | loop fusion | bytes 1048576 | tf_op jit(solution)/shard_map/reshape | solution.py:607
  109.9 0.0 slice-done
  109.9 0.3 reshape_squeeze.3
  110.2 0.1 pad_maximum_fusion
  110.3 1.1 %copy.25 = f32[160,4,256]{2,1,0:T(4,128)} copy(f32[160,4,256]{0,2,1:T(8,128)S(1)} %pad_maximum_fusion) | data formatting | bytes 1310720 | tf_op jit(solution)/shard_map/concatenate | solution.py:609
  (21 shorter events, 0.3 us)
Async XLA Ops:
  0.0 0.7 copy-start.4
  0.7 0.7 copy-start.2
  0.7 0.7 copy-start.3
  1.4 46.9 %collective-permute-start = (f32[4,128]{1,0:T(4,128)S(1)}, f32[4,128]{1,0:T(4,128)S(1)}, u32[]{:S(2)}, u32[]{:S(2)}) collective-permute-start(f32[4,128]{1,0:T(4,128)S(1)} %select_maximum_fusion.1), channel_id=1, source_target_pairs={{0,0},{1,8},{2,16},{3,24},{4,26},{5,18},{6,10},{7,2},{8,4},{9,12},... | collective-permute-start | bytes 6152 | tf_op jit(solution)/shard_map/ppermute | solution.py:518
  3.5 0.7 copy-start.1
  4.7 0.9 copy-start
  108.7 1.1 %slice-start = ((f32[32,5,8,128]{3,2,1,0:T(8,128)}), f32[32,1,8,128]{3,2,1,0:T(8,128)S(1)}, s32[]{:S(2)}) async-start(f32[32,5,8,128]{3,2,1,0:T(8,128)} %shard_map.71), calls=%async_computation | async-start | bytes 262144 | tf_op jit(solution)/shard_map/slice | solution.py:608
